TPU v7x, 32 devices: a whole 2x2x4 slice. The times are simulated.
32 devices in a mesh: dp: 2 (over core), gx: 4 (over y, x), gy: 4 (over z).
Axes of the slice: x: 2, y: 2, z: 4, core: 2. Of those that a mesh axis runs over, the one named last changes fastest.
Arguments:
- volume: bfloat16 [2, 4, 8, 32, 128], P('dp', None, 'gx', 'gy'), may hold values from -6 to 6
- targets: float32 [2, 4], P('dp'), may hold values from -4 to 4
- conv1_w: bfloat16 [27, 128], replicated, may hold values from -0.625 to 0.625
- conv1_b: float32 [32], replicated, may hold values from -3 to 3
- conv2_w: bfloat16 [27, 2048], replicated, may hold values from -0.21875 to 0.21875
- conv2_b: float32 [64], replicated, may hold values from -3 to 3
- head_w: float32 [64, 4], replicated, may hold values from -2 to 2
- head_b: float32 [4], replicated, may hold values from -4 to 4
- dir1: float32 [27, 128], replicated, may hold values from -6 to 6
- dir2: float32 [27, 2048], replicated, may hold values from -1.2 to 1.2
- dir_head: float32 [64, 4], replicated, may hold values from -6 to 6
Outputs:
- next1: float32 [27, 128], replicated
- next2: float32 [27, 2048], replicated
- next_head: float32 [64, 4], replicated
- rayleigh: float32 [], replicated
- curvature_field: float32 [2, 32, 8, 32, 128], P('dp', None, 'gx', 'gy')
All inputs are finite; a program needn't handle non-finite values.
Results may differ from a plain program's by a relative error of at most 0.0051.
Values may be sent and summed in bfloat16 or wider, within the bound.
A program may use at most 128 MiB of HBM per device.

v0:
```python
import jax
import jax.numpy as jnp
from jax import lax
from jax.experimental import pallas as pl
from jax.experimental.pallas import tpu as pltpu
from jax.sharding import PartitionSpec as P

C0 = 4
C1 = 32
C2 = 64
ROWS = 16
F32 = jnp.float32
BF16 = jnp.bfloat16


def extended(cells, sides, width):
    for axis, dim in sides:
        count = lax.axis_size(axis)
        ends = count - 1
        head = lax.slice_in_dim(cells, 0, width, axis=dim)
        tail = lax.slice_in_dim(cells, cells.shape[dim] - width, cells.shape[dim], axis=dim)
        cells = jnp.concatenate(
            [
                lax.ppermute(tail, axis, [(i, (i + 1) % count) for i in range(ends)]),
                cells,
                lax.ppermute(head, axis, [((i + 1) % count, i) for i in range(ends)]),
            ],
            axis=dim,
        )
    return cells


def swapped_sum(u, axis):
    count = lax.axis_size(axis)
    if count & (count - 1):
        return lax.psum(u, axis)
    step = 1
    while step < count:
        u = u + lax.ppermute(u, axis, [(i, i ^ step) for i in range(count)])
        step *= 2
    return u


def swapped(u, axis):
    return lax.ppermute(u, axis, [(0, 1), (1, 0)])


def total_sum(u):
    if lax.axis_size("dp") != 2:
        return lax.psum(u, ("dp", "gx", "gy"))
    half = u.shape[0] // 2
    me = lax.axis_index("dp")
    mine = lax.dynamic_slice_in_dim(u, me * half, half, 0)
    other = lax.dynamic_slice_in_dim(u, (1 - me) * half, half, 0)
    mine = mine + swapped(other, "dp")
    mine = swapped_sum(swapped_sum(mine, "gx"), "gy")
    other = swapped(mine, "dp")
    first = me == 0
    return jnp.concatenate([jnp.where(first, mine, other), jnp.where(first, other, mine)], axis=0)


def silu_parts(z):
    s = 1.0 / (1.0 + jnp.exp(-z))
    return (z * s, s * (1.0 + z * (1.0 - s)), s * (1.0 - s) * (2.0 + z * (1.0 - 2.0 * s)))


def window(ref, x, y, count):
    columns = []
    for k in range(count):
        parts = []
        for a in range(3):
            rows = ref[x + a, y + k : y + k + 3]
            parts.append(rows.reshape(rows.shape[0] * rows.shape[1], rows.shape[2]))
        columns.append(jnp.concatenate(parts, axis=0))
    return jnp.concatenate(columns, axis=1)


def lane_of(shape):
    return lax.broadcasted_iota(jnp.int32, shape, 1)


def from_left(u):
    return jnp.where(lane_of(u.shape) == 0, 0.0, pltpu.roll(u, 1, 1))


def from_right(u):
    last = u.shape[1] - 1
    return jnp.where(lane_of(u.shape) == last, 0.0, pltpu.roll(u, last, 1))


def gathered(y, n):
    return from_left(y[:n]) + y[n : 2 * n] + from_right(y[2 * n : 3 * n])


def forward_kernel(v_ref, l1_ref, b1_ref, l2_ref, b2_ref, pq_ref, a_ref, ta_ref, d_ref, pool_ref):
    nx, ny, lanes = (pq_ref.shape[1], pq_ref.shape[2], pq_ref.shape[4])
    b1 = b1_ref[...]
    l1 = l1_ref[...]
    for x in range(nx + 2):
        for y in range(0, ny + 2, 2):
            res = jnp.dot(l1, window(v_ref, x, y, 2), preferred_element_type=F32)
            for k in range(2):
                part = res[:, k * lanes : (k + 1) * lanes]
                z1 = part[:C1] + b1
                t1 = part[C1:]
                mask = v_ref[x + 1, y + k + 1].astype(F32)[3 * C0 : 3 * C0 + 1]
                act, slope, bend = silu_parts(z1)
                a_ref[x, y + k] = (act * mask).astype(BF16)
                ta_ref[x, y + k] = (slope * t1 * mask).astype(BF16)
                if 1 <= x <= nx and 1 <= y + k <= ny:
                    d_ref[0, x - 1, y + k - 1] = slope.astype(BF16)
                    d_ref[1, x - 1, y + k - 1] = (bend * t1).astype(BF16)
    b2 = b2_ref[...]
    n = 3 * C2
    total = jnp.zeros((C2, lanes), F32)
    ttotal = jnp.zeros((C2, lanes), F32)
    for x in range(nx):
        for y in range(0, ny, 2):
            res = jnp.dot(l2_ref[...], window(a_ref, x, y, 2), preferred_element_type=F32)
            tres = res[n:] + jnp.dot(l2_ref[:n], window(ta_ref, x, y, 2), preferred_element_type=F32)
            for k in range(2):
                z2 = gathered(res[:n, k * lanes : (k + 1) * lanes], C2) + b2
                t2 = gathered(tres[:, k * lanes : (k + 1) * lanes], C2)
                act, slope, bend = silu_parts(z2)
                total = total + act
                ttotal = ttotal + slope * t2
                pq_ref[0, x, y + k] = slope.astype(BF16)
                pq_ref[1, x, y + k] = (bend * t2).astype(BF16)
    both = (jnp.sum(total, axis=1, keepdims=True), jnp.sum(ttotal, axis=1, keepdims=True))
    pool_ref[...] = jnp.where(lane_of(pool_ref.shape) == 0, both[0], both[1])


NT = (((1,), (1,)), ((), ()))


def backward_kernel(
    cells, batch, pq_ref, a_ref, ta_ref, d_ref, v_ref, lb_ref, pool_ref, targets_ref,
    head_w_ref, head_b_ref, dir_head_ref, h_ref, hd_ref, field_ref, g_ref, tg_ref,
):
    nx, ny, lanes = (d_ref.shape[1], d_ref.shape[2], d_ref.shape[4])
    pooled = pool_ref[:, 0:1] / cells
    tpooled = pool_ref[:, 1:2] / cells
    head_w = head_w_ref[...]
    dir_head = dir_head_ref[...]
    out = jnp.sum(pooled * head_w, axis=0, keepdims=True) + head_b_ref[...]
    tout = jnp.sum(tpooled * head_w + pooled * dir_head, axis=0, keepdims=True)
    dy = (out - targets_ref[...]) / batch
    tdy = tout / batch
    hd_ref[...] = tpooled * dy + pooled * tdy
    dpool = jnp.sum(dy * head_w, axis=1, keepdims=True) / cells
    tdpool = jnp.sum(tdy * head_w + dy * dir_head, axis=1, keepdims=True) / cells
    for x in range(nx + 2):
        for y in range(ny + 2):
            slope = pq_ref[0, x, y].astype(F32)
            bent = pq_ref[1, x, y].astype(F32)
            g_ref[x, y] = (slope * dpool).astype(BF16)
            tg_ref[x, y] = (bent * dpool + slope * tdpool).astype(BF16)

    def moved(ref, x, y):
        columns = []
        for k in range(2):
            u = ref[x + 1, y + k + 1].astype(F32)
            columns.append(jnp.concatenate([from_right(u), u, from_left(u)], axis=0).astype(BF16))
        return jnp.concatenate(columns, axis=1)

    cut = 8 * C1
    most = jnp.zeros((3 * C2, cut), F32)
    rest = jnp.zeros((C1, 3 * C2), F32)
    for x in range(nx):
        for y in range(0, ny, 2):
            for grads, cells_ref in ((tg_ref, a_ref), (g_ref, ta_ref)):
                g = moved(grads, x, y)
                u = window(cells_ref, x, y, 2)
                most = most + lax.dot_general(g, u[:cut], NT, preferred_element_type=F32)
                rest = rest + lax.dot_general(u[cut:], g, NT, preferred_element_type=F32)
    top = 3 * C2
    h_ref[:top, :] = most
    h_ref[top:, :] = jnp.zeros((2 * C1, cut), F32)
    h_ref[top : top + C1, : 3 * C2] = rest
    n = 3 * C1
    h1 = jnp.zeros((C1, 9 * ROWS), F32)
    for x in range(nx):
        for y in range(0, ny, 2):
            res = jnp.dot(lb_ref[...], window(g_ref, x, y, 2), preferred_element_type=F32)
            tres = res[n:] + jnp.dot(lb_ref[:n], window(tg_ref, x, y, 2), preferred_element_type=F32)
            grads = []
            for k in range(2):
                da = gathered(res[:n, k * lanes : (k + 1) * lanes], C1)
                tda = gathered(tres[:, k * lanes : (k + 1) * lanes], C1)
                field_ref[:, x, y + k, :] = tda * cells
                grads.append((d_ref[1, x, y + k].astype(F32) * da + d_ref[0, x, y + k].astype(F32) * tda).astype(BF16))
            h1 = h1 + lax.dot_general(
                jnp.concatenate(grads, axis=1), window(v_ref, x + 1, y + 1, 2), NT, preferred_element_type=F32
            )
    h_ref[top + C1 :, : 9 * ROWS] = h1


def vmem_call(kernel, shapes, scratch=()):
    return pl.pallas_call(
        kernel,
        out_shape=shapes,
        scratch_shapes=scratch,
        compiler_params=pltpu.CompilerParams(vmem_limit_bytes=48 * 1024 * 1024),
    )


def per_device(
    volume, targets, conv1_w, conv1_b, conv2_w, conv2_b, head_w, head_b, dir1, dir2, dir_head
):
    nx, ny, lanes = volume.shape[2:]
    cells = nx * lax.axis_size("gx") * ny * lax.axis_size("gy") * lanes
    batch = volume.shape[0] * lax.axis_size("dp")
    rows = volume[0].transpose(1, 2, 0, 3)
    wide = jnp.pad(rows, ((0, 0), (0, 0), (0, 0), (1, 1)))
    v = jnp.concatenate(
        [wide[..., :lanes], rows, wide[..., 2:], jnp.ones((nx, ny, 1, lanes), BF16), jnp.zeros((nx, ny, 3, lanes), BF16)],
        axis=2,
    )
    v = extended(v, (("gx", 0), ("gy", 1)), 2)
    first = jnp.stack((conv1_w, dir1.astype(BF16))).reshape(2, 9, 3, C1, C0)
    first = first.transpose(0, 3, 1, 2, 4).reshape(2 * C1, 9, 3 * C0)
    l1 = jnp.pad(first, ((0, 0), (0, 0), (0, ROWS - 3 * C0))).reshape(2 * C1, 9 * ROWS)
    second = jnp.stack((conv2_w, dir2.astype(BF16))).reshape(2, 9, 3, C2, C1)
    l2 = second.transpose(0, 2, 3, 1, 4).reshape(6 * C2, 9 * C1)
    lb = jnp.flip(second, (1, 2)).transpose(0, 2, 4, 1, 3).reshape(6 * C1, 9 * C2)
    shape = jax.ShapeDtypeStruct
    pq, a1, ta1, d, pool = vmem_call(
        forward_kernel,
        (
            shape((2, nx, ny, C2, lanes), BF16),
            shape((nx + 2, ny + 2, C1, lanes), BF16),
            shape((nx + 2, ny + 2, C1, lanes), BF16),
            shape((2, nx, ny, C1, lanes), BF16),
            shape((C2, 2), F32),
        ),
    )(v, l1, conv1_b[:, None], l2, conv2_b[:, None])
    pool = swapped_sum(swapped_sum(pool, "gx"), "gy")
    pq = extended(pq, (("gx", 1), ("gy", 2)), 1)

    def backward(*refs):
        backward_kernel(cells, batch, *refs)

    h, hd, field = vmem_call(
        backward,
        (
            shape((3 * C2 + 2 * C1, 8 * C1), F32),
            shape((C2, head_w.shape[1]), F32),
            shape((C1, nx, ny, lanes), F32),
        ),
        (
            pltpu.VMEM((nx + 2, ny + 2, C2, lanes), BF16),
            pltpu.VMEM((nx + 2, ny + 2, C2, lanes), BF16),
        ),
    )(pq, a1, ta1, d, v, lb, pool, targets, head_w, head_b[None], dir_head)
    hd = swapped_sum(hd, "dp")
    h = total_sum(h)
    top = 3 * C2
    most = h[:top].reshape(3, C2, 8, C1).transpose(2, 0, 1, 3).reshape(24, C2 * C1)
    rest = h[top : top + C1, :top].reshape(C1, 3, C2).transpose(1, 2, 0).reshape(3, C2 * C1)
    h2 = jnp.concatenate([most, rest], axis=0)
    h1 = h[top + C1 :, : 9 * ROWS].reshape(C1, 9, ROWS)[:, :, : 3 * C0]
    h1 = h1.reshape(C1, 27, C0).transpose(1, 0, 2).reshape(27, C1 * C0)
    quad = jnp.sum(dir1 * h1) + jnp.sum(dir2 * h2) + jnp.sum(dir_head * hd)
    length = jnp.sum(dir1 * dir1) + jnp.sum(dir2 * dir2) + jnp.sum(dir_head * dir_head)
    nrm = jnp.sqrt(jnp.sum(h1 * h1) + jnp.sum(h2 * h2) + jnp.sum(hd * hd) + 1e-06)
    return (h1 / nrm, h2 / nrm, hd / nrm, quad / length, field[None])


def solution(mesh):
    return jax.shard_map(
        per_device,
        mesh=mesh,
        in_specs=(P("dp", None, "gx", "gy", None), P("dp", None)) + (P(),) * 9,
        out_specs=(P(), P(), P(), P(), P("dp", None, "gx", "gy", None)),
        check_vma=False,
    )
```

profile of v0, /device:TPU:0, one launch (start us, length us, event | category | flops | bytes accessed | tf_op | source)
XLA Modules:
  0.0 102.5 jit_solution(13493882081988508141)
XLA Ops:
  1.6 1.3 %collective-permute-start.1 = (bf16[2,8,16,128]{3,2,1,0:T(8,128)(2,1)S(1)}, bf16[2,8,16,128]{3,2,1,0:T(8,128)(2,1)S(1)}, u32[]{:S(2)}, u32[]{:S(2)}) collective-permute-start(bf16[2,8,16,128]{3,2,1,0:T(8,128)(2,1)S(1)} %concatenate.23), channel_id=1, source_target_pairs={{4,0},{8,4},{12,8},{5,1},{9,5},{13,9},{6,2},{10,6},{14,10},{7,3},{... | collective-permute-start | bytes 196616 | tf_op jit(solution)/shard_map/ppermute | solution.py:26
  2.9 5.5 %collective-permute-start = (bf16[2,8,16,128]{3,2,1,0:T(8,128)(2,1)S(1)}, bf16[2,8,16,128]{3,2,1,0:T(8,128)(2,1)S(1)}, u32[]{:S(2)}, u32[]{:S(2)}) collective-permute-start(bf16[2,8,16,128]{3,2,1,0:T(8,128)(2,1)S(1)} %concatenate.23), channel_id=1, source_target_pairs={{0,4},{4,8},{8,12},{1,5},{5,9},{9,13},{2,6},{6,10},{10,14},{3,7},{... | collective-permute-start | bytes 196616 | tf_op jit(solution)/shard_map/ppermute | solution.py:24
  8.4 1.4 %multiply_reduce_fusion.7 = (f32[]{:T(128)}, bf16[27,128]{1,0:T(8,128)(2,1)S(1)}) fusion(f32[27,128]{1,0:T(8,128)} %param.19), kind=kLoop, calls=%fused_computation.30 | loop fusion | flops 10367 | bytes 20740 | tf_op jit(solution)/shard_map/reduce_sum | solution.py:264
  13.8 4.0 %collective-permute-start.2 = (bf16[6,2,16,128]{3,2,1,0:T(8,128)(2,1)S(1)}, bf16[6,2,16,128]{3,2,1,0:T(8,128)(2,1)S(1)}, u32[]{:S(2)}, u32[]{:S(2)}) collective-permute-start(bf16[6,2,16,128]{3,2,1,0:T(8,128)(2,1)S(1)} %get-tuple-element.48), channel_id=1, source_target_pairs={{0,1},{1,2},{2,3},{4,5},{5,6},{6,7},{8,9},{9,10},{10,11},{12,13},{... | collective-permute-start | bytes 147464 | tf_op jit(solution)/shard_map/ppermute | solution.py:24
  17.8 1.3 %collective-permute-start.3 = (bf16[6,2,16,128]{3,2,1,0:T(8,128)(2,1)S(1)}, bf16[6,2,16,128]{3,2,1,0:T(8,128)(2,1)S(1)}, u32[]{:S(2)}, u32[]{:S(2)}) collective-permute-start(bf16[6,2,16,128]{3,2,1,0:T(8,128)(2,1)S(1)} %get-tuple-element.49), channel_id=1, source_target_pairs={{1,0},{2,1},{3,2},{5,4},{6,5},{7,6},{9,8},{10,9},{11,10},{13,12},{... | collective-permute-start | bytes 147464 | tf_op jit(solution)/shard_map/ppermute | solution.py:26
  21.0 2.8 %collective-permute-done.3 = bf16[6,2,16,128]{3,2,1,0:T(8,128)(2,1)S(1)} collective-permute-done((bf16[6,2,16,128]{3,2,1,0:T(8,128)(2,1)S(1)}, bf16[6,2,16,128]{3,2,1,0:T(8,128)(2,1)S(1)}, u32[]{:S(2)}, u32[]{:S(2)}) %collective-permute-start.3) | collective-permute-done | bytes 49184 | tf_op jit(solution)/shard_map/ppermute | solution.py:26
  23.8 2.0 %shard_map.146 = (bf16[2,2,8,64,128]{4,3,2,1,0:T(8,128)(2,1)S(1)}, bf16[4,10,32,128]{3,2,1,0:T(8,128)(2,1)S(1)}, bf16[4,10,32,128]{3,2,1,0:T(8,128)(2,1)S(1)}, b...) custom-call(bf16[6,12,16,128]{3,2,1,0:T(8,128)(2,1)S(1)} %pad_maximum_fusion.1.v_ref.refs_4_, ...), custom_call_target="tpu_custom_call" | custom-call | tf_op jit(solution)/shard_map/pallas_call | solution.py:227
  25.9 4.3 %collective-permute-start.4 = (bf16[2,1,8,64,128]{4,3,2,1,0:T(8,128)(2,1)S(1)}, bf16[2,1,8,64,128]{4,3,2,1,0:T(8,128)(2,1)S(1)}, u32[]{:S(2)}, u32[]{:S(2)}) collective-permute-start(bf16[2,1,8,64,128]{4,3,2,1,0:T(8,128)(2,1)S(1)} %get-tuple-element.45), channel_id=1, source_target_pairs={{0,4},{4,8},{8,12},{1,5},{5,9},{9,13},{2,6},{6,10},{10,14},{3,7},{... | collective-permute-start | bytes 786440 | tf_op jit(solution)/shard_map/ppermute | solution.py:24
  31.5 2.7 %collective-permute-start.8 = (f32[64,2]{1,0:T(8,128)S(1)}, f32[64,2]{1,0:T(8,128)S(1)}, u32[]{:S(2)}, u32[]{:S(2)}) collective-permute-start(f32[64,2]{1,0:T(8,128)S(1)} %get-tuple-element.17), channel_id=1, source_target_pairs={{0,4},{4,0},{8,12},{12,8},{1,5},{5,1},{9,13},{13,9},{2,6},{6,2},{1... | collective-permute-start | bytes 1544 | tf_op jit(solution)/shard_map/ppermute | solution.py:39
  34.2 7.2 %collective-permute-done.8 = f32[64,2]{1,0:T(8,128)S(1)} collective-permute-done((f32[64,2]{1,0:T(8,128)S(1)}, f32[64,2]{1,0:T(8,128)S(1)}, u32[]{:S(2)}, u32[]{:S(2)}) %collective-permute-start.8) | collective-permute-done | bytes 544 | tf_op jit(solution)/shard_map/ppermute | solution.py:39
  42.3 3.5 %collective-permute-start.6 = (bf16[2,4,1,64,128]{4,3,2,1,0:T(8,128)(2,1)}, bf16[2,4,1,64,128]{4,3,2,1,0:T(8,128)(2,1)S(1)}, u32[]{:S(2)}, u32[]{:S(2)}) collective-permute-start(bf16[2,4,1,64,128]{4,3,2,1,0:T(8,128)(2,1)} %get-tuple-element.42), channel_id=1, source_target_pairs={{0,1},{1,2},{2,3},{4,5},{5,6},{6,7},{8,9},{9,10},{10,11},{12,13},{... | collective-permute-start | bytes 393224 | tf_op jit(solution)/shard_map/ppermute | solution.py:24
  47.2 2.7 %collective-permute-start.10 = (f32[64,2]{1,0:T(8,128)S(1)}, f32[64,2]{1,0:T(8,128)S(1)}, u32[]{:S(2)}, u32[]{:S(2)}) collective-permute-start(f32[64,2]{1,0:T(8,128)S(1)} %add.62), channel_id=1, source_target_pairs={{0,1},{1,0},{2,3},{3,2},{4,5},{5,4},{6,7},{7,6},{8,9},{9,8},{10,11... | collective-permute-start | bytes 1544 | tf_op jit(solution)/shard_map/ppermute | solution.py:39
  49.9 3.6 %collective-permute-done.10 = f32[64,2]{1,0:T(8,128)S(1)} collective-permute-done((f32[64,2]{1,0:T(8,128)S(1)}, f32[64,2]{1,0:T(8,128)S(1)}, u32[]{:S(2)}, u32[]{:S(2)}) %collective-permute-start.10) | collective-permute-done | bytes 544 | tf_op jit(solution)/shard_map/ppermute | solution.py:39
  53.5 1.5 %collective-permute-start.11 = (f32[64,2]{1,0:T(8,128)S(1)}, f32[64,2]{1,0:T(8,128)S(1)}, u32[]{:S(2)}, u32[]{:S(2)}) collective-permute-start(f32[64,2]{1,0:T(8,128)S(1)} %add.63), channel_id=1, source_target_pairs={{0,2},{1,3},{2,0},{3,1},{4,6},{5,7},{6,4},{7,5},{8,10},{9,11},{10,... | collective-permute-start | bytes 1544 | tf_op jit(solution)/shard_map/ppermute | solution.py:39
  56.5 1.9 %collective-permute-done.11 = f32[64,2]{1,0:T(8,128)S(1)} collective-permute-done((f32[64,2]{1,0:T(8,128)S(1)}, f32[64,2]{1,0:T(8,128)S(1)}, u32[]{:S(2)}, u32[]{:S(2)}) %collective-permute-start.11) | collective-permute-done | bytes 544 | tf_op jit(solution)/shard_map/ppermute | solution.py:39
  58.5 1.4 %pad_maximum_fusion.refs_0_ = bf16[2,4,10,64,128]{4,3,2,1,0:T(8,128)(2,1)S(1)} fusion(bf16[2,4,1,64,128]{4,3,2,1,0:T(8,128)(2,1)S(1)} %collective-permute-done.7, bf16[2,4,8,64,128]{4,3,2,1,0:T(8,128)(2,1)} %copy-done.2, bf16[2,4,1,64,128]{4,3,2,1,0:T(8,128)(2,1)S(1)} %collective-permute-done.6), kind=kLoop, calls=%fused_computation | loop fusion | flops 1310720 | bytes 2621440 | tf_op jit(solution)/shard_map/concatenate | solution.py:22
  59.9 4.2 %shard_map.147 = (f32[256,256]{1,0:T(8,128)S(1)}, f32[64,4]{1,0:T(8,128)S(1)}, f32[32,2,8,128]{3,2,1,0:T(8,128)}) custom-call(bf16[2,4,10,64,128]{4,3,2,1,0:T(8,128)(2,1)S(1)} %pad_maximum_fusion.refs_0_, bf16[4,10,32,128]{3,2,1,0:T(8,128)(2,1)S(1)} %get-tuple-element.14.refs_1_, bf16[4,10,32,128]{3,2,1,0:T(8,128)(2,1)S(1)} %get-tuple-element.15.refs_2_, ...), custom_call_target="tpu_custom_call" | custom-call | tf_op jit(solution)/shard_map/pallas_call | solution.py:243
  64.2 1.3 %collective-permute-done.12 = f32[128,256]{1,0:T(8,128)S(1)} collective-permute-done((f32[128,256]{1,0:T(8,128)S(1)}, f32[128,256]{1,0:T(8,128)S(1)}, u32[]{:S(2)}, u32[]{:S(2)}) %collective-permute-start.12) | collective-permute-done | bytes 131104 | tf_op jit(solution)/shard_map/ppermute | solution.py:45
  66.2 4.9 %collective-permute-done.13 = f32[128,256]{1,0:T(8,128)S(1)} collective-permute-done((f32[128,256]{1,0:T(8,128)S(1)}, f32[128,256]{1,0:T(8,128)S(1)}, u32[]{:S(2)}, u32[]{:S(2)}) %collective-permute-start.13) | collective-permute-done | bytes 131104 | tf_op jit(solution)/shard_map/ppermute | solution.py:39
  71.2 2.1 %collective-permute-start.14 = (f32[128,256]{1,0:T(8,128)S(1)}, f32[128,256]{1,0:T(8,128)S(1)}, u32[]{:S(2)}, u32[]{:S(2)}) collective-permute-start(f32[128,256]{1,0:T(8,128)S(1)} %add.68), channel_id=1, source_target_pairs={{0,8},{4,12},{8,0},{12,4},{1,9},{5,13},{9,1},{13,5},{2,10},{6,14},... | collective-permute-start | bytes 393224 | tf_op jit(solution)/shard_map/ppermute | solution.py:39
  73.3 3.0 %collective-permute-done.14 = f32[128,256]{1,0:T(8,128)S(1)} collective-permute-done((f32[128,256]{1,0:T(8,128)S(1)}, f32[128,256]{1,0:T(8,128)S(1)}, u32[]{:S(2)}, u32[]{:S(2)}) %collective-permute-start.14) | collective-permute-done | bytes 131104 | tf_op jit(solution)/shard_map/ppermute | solution.py:39
  76.6 4.8 %collective-permute-done.15 = f32[128,256]{1,0:T(8,128)S(1)} collective-permute-done((f32[128,256]{1,0:T(8,128)S(1)}, f32[128,256]{1,0:T(8,128)S(1)}, u32[]{:S(2)}, u32[]{:S(2)}) %collective-permute-start.15) | collective-permute-done | bytes 131104 | tf_op jit(solution)/shard_map/ppermute | solution.py:39
  81.3 1.5 %collective-permute-start.16 = (f32[128,256]{1,0:T(8,128)S(1)}, f32[128,256]{1,0:T(8,128)S(1)}, u32[]{:S(2)}, u32[]{:S(2)}) collective-permute-start(f32[128,256]{1,0:T(8,128)S(1)} %add.70), channel_id=1, source_target_pairs={{0,2},{1,3},{2,0},{3,1},{4,6},{5,7},{6,4},{7,5},{8,10},{9,11},{10,... | collective-permute-start | bytes 393224 | tf_op jit(solution)/shard_map/ppermute | solution.py:39
  83.6 4.8 %collective-permute-done.16 = f32[128,256]{1,0:T(8,128)S(1)} collective-permute-done((f32[128,256]{1,0:T(8,128)S(1)}, f32[128,256]{1,0:T(8,128)S(1)}, u32[]{:S(2)}, u32[]{:S(2)}) %collective-permute-start.16) | collective-permute-done | bytes 131104 | tf_op jit(solution)/shard_map/ppermute | solution.py:39
  (110 shorter events, 20.9 us)
Async XLA Ops:
  0.6 12.7 %copy-start.4 = (bf16[27,2048]{1,0:T(8,128)(2,1)S(1)}, bf16[27,2048]{1,0:T(8,128)(2,1)}, u32[]{:S(2)}) copy-start(bf16[27,2048]{1,0:T(8,128)(2,1)} %param.15) | copy-start | bytes 331780
  1.6 12.1 %collective-permute-start.1 = (bf16[2,8,16,128]{3,2,1,0:T(8,128)(2,1)S(1)}, bf16[2,8,16,128]{3,2,1,0:T(8,128)(2,1)S(1)}, u32[]{:S(2)}, u32[]{:S(2)}) collective-permute-start(bf16[2,8,16,128]{3,2,1,0:T(8,128)(2,1)S(1)} %concatenate.23), channel_id=1, source_target_pairs={{4,0},{8,4},{12,8},{5,1},{9,5},{13,9},{6,2},{10,6},{14,10},{7,3},{... | collective-permute-start | bytes 196616 | tf_op jit(solution)/shard_map/ppermute | solution.py:26
  2.9 10.9 %collective-permute-start = (bf16[2,8,16,128]{3,2,1,0:T(8,128)(2,1)S(1)}, bf16[2,8,16,128]{3,2,1,0:T(8,128)(2,1)S(1)}, u32[]{:S(2)}, u32[]{:S(2)}) collective-permute-start(bf16[2,8,16,128]{3,2,1,0:T(8,128)(2,1)S(1)} %concatenate.23), channel_id=1, source_target_pairs={{0,4},{4,8},{8,12},{1,5},{5,9},{9,13},{2,6},{6,10},{10,14},{3,7},{... | collective-permute-start | bytes 196616 | tf_op jit(solution)/shard_map/ppermute | solution.py:24
  13.3 6.0 %copy-start.8 = (f32[64]{0:T(128)S(1)}, f32[64]{0:T(128)}, u32[]{:S(2)}) copy-start(f32[64]{0:T(128)} %param.16) | copy-start | bytes 772
  13.8 7.2 %collective-permute-start.2 = (bf16[6,2,16,128]{3,2,1,0:T(8,128)(2,1)S(1)}, bf16[6,2,16,128]{3,2,1,0:T(8,128)(2,1)S(1)}, u32[]{:S(2)}, u32[]{:S(2)}) collective-permute-start(bf16[6,2,16,128]{3,2,1,0:T(8,128)(2,1)S(1)} %get-tuple-element.48), channel_id=1, source_target_pairs={{0,1},{1,2},{2,3},{4,5},{5,6},{6,7},{8,9},{9,10},{10,11},{12,13},{... | collective-permute-start | bytes 147464 | tf_op jit(solution)/shard_map/ppermute | solution.py:24
  17.8 6.0 %collective-permute-start.3 = (bf16[6,2,16,128]{3,2,1,0:T(8,128)(2,1)S(1)}, bf16[6,2,16,128]{3,2,1,0:T(8,128)(2,1)S(1)}, u32[]{:S(2)}, u32[]{:S(2)}) collective-permute-start(bf16[6,2,16,128]{3,2,1,0:T(8,128)(2,1)S(1)} %get-tuple-element.49), channel_id=1, source_target_pairs={{1,0},{2,1},{3,2},{5,4},{6,5},{7,6},{9,8},{10,9},{11,10},{13,12},{... | collective-permute-start | bytes 147464 | tf_op jit(solution)/shard_map/ppermute | solution.py:26
  25.9 15.5 %collective-permute-start.4 = (bf16[2,1,8,64,128]{4,3,2,1,0:T(8,128)(2,1)S(1)}, bf16[2,1,8,64,128]{4,3,2,1,0:T(8,128)(2,1)S(1)}, u32[]{:S(2)}, u32[]{:S(2)}) collective-permute-start(bf16[2,1,8,64,128]{4,3,2,1,0:T(8,128)(2,1)S(1)} %get-tuple-element.45), channel_id=1, source_target_pairs={{0,4},{4,8},{8,12},{1,5},{5,9},{9,13},{2,6},{6,10},{10,14},{3,7},{... | collective-permute-start | bytes 786440 | tf_op jit(solution)/shard_map/ppermute | solution.py:24
  30.2 11.3 %collective-permute-start.5 = (bf16[2,1,8,64,128]{4,3,2,1,0:T(8,128)(2,1)S(1)}, bf16[2,1,8,64,128]{4,3,2,1,0:T(8,128)(2,1)S(1)}, u32[]{:S(2)}, u32[]{:S(2)}) collective-permute-start(bf16[2,1,8,64,128]{4,3,2,1,0:T(8,128)(2,1)S(1)} %get-tuple-element.44), channel_id=1, source_target_pairs={{4,0},{8,4},{12,8},{5,1},{9,5},{13,9},{6,2},{10,6},{14,10},{7,3},{... | collective-permute-start | bytes 786440 | tf_op jit(solution)/shard_map/ppermute | solution.py:26
  31.5 9.9 %collective-permute-start.8 = (f32[64,2]{1,0:T(8,128)S(1)}, f32[64,2]{1,0:T(8,128)S(1)}, u32[]{:S(2)}, u32[]{:S(2)}) collective-permute-start(f32[64,2]{1,0:T(8,128)S(1)} %get-tuple-element.17), channel_id=1, source_target_pairs={{0,4},{4,0},{8,12},{12,8},{1,5},{5,1},{9,13},{13,9},{2,6},{6,2},{1... | collective-permute-start | bytes 1544 | tf_op jit(solution)/shard_map/ppermute | solution.py:39
  41.4 5.8 %collective-permute-start.9 = (f32[64,2]{1,0:T(8,128)S(1)}, f32[64,2]{1,0:T(8,128)S(1)}, u32[]{:S(2)}, u32[]{:S(2)}) collective-permute-start(f32[64,2]{1,0:T(8,128)S(1)} %add.61), channel_id=1, source_target_pairs={{0,8},{4,12},{8,0},{12,4},{1,9},{5,13},{9,1},{13,5},{2,10},{6,14},... | collective-permute-start | bytes 1544 | tf_op jit(solution)/shard_map/ppermute | solution.py:39
  41.6 13.5 %copy-start.6 = (f32[64,4]{0,1:T(4,128)S(1)}, f32[64,4]{0,1:T(4,128)}, u32[]{:S(2)}) copy-start(f32[64,4]{0,1:T(4,128)} %param.21) | copy-start | bytes 3076
  41.6 13.6 %copy-start.7 = (f32[64,4]{0,1:T(4,128)S(1)}, f32[64,4]{0,1:T(4,128)}, u32[]{:S(2)}) copy-start(f32[64,4]{0,1:T(4,128)} %param.17) | copy-start | bytes 3076
  42.3 16.1 %collective-permute-start.6 = (bf16[2,4,1,64,128]{4,3,2,1,0:T(8,128)(2,1)}, bf16[2,4,1,64,128]{4,3,2,1,0:T(8,128)(2,1)S(1)}, u32[]{:S(2)}, u32[]{:S(2)}) collective-permute-start(bf16[2,4,1,64,128]{4,3,2,1,0:T(8,128)(2,1)} %get-tuple-element.42), channel_id=1, source_target_pairs={{0,1},{1,2},{2,3},{4,5},{5,6},{6,7},{8,9},{9,10},{10,11},{12,13},{... | collective-permute-start | bytes 393224 | tf_op jit(solution)/shard_map/ppermute | solution.py:24
  45.8 12.7 %collective-permute-start.7 = (bf16[2,4,1,64,128]{4,3,2,1,0:T(8,128)(2,1)}, bf16[2,4,1,64,128]{4,3,2,1,0:T(8,128)(2,1)S(1)}, u32[]{:S(2)}, u32[]{:S(2)}) collective-permute-start(bf16[2,4,1,64,128]{4,3,2,1,0:T(8,128)(2,1)} %get-tuple-element.43), channel_id=1, source_target_pairs={{1,0},{2,1},{3,2},{5,4},{6,5},{7,6},{9,8},{10,9},{11,10},{13,12},{... | collective-permute-start | bytes 393224 | tf_op jit(solution)/shard_map/ppermute | solution.py:26
  47.2 6.3 %collective-permute-start.10 = (f32[64,2]{1,0:T(8,128)S(1)}, f32[64,2]{1,0:T(8,128)S(1)}, u32[]{:S(2)}, u32[]{:S(2)}) collective-permute-start(f32[64,2]{1,0:T(8,128)S(1)} %add.62), channel_id=1, source_target_pairs={{0,1},{1,0},{2,3},{3,2},{4,5},{5,4},{6,7},{7,6},{8,9},{9,8},{10,11... | collective-permute-start | bytes 1544 | tf_op jit(solution)/shard_map/ppermute | solution.py:39
  53.5 4.9 %collective-permute-start.11 = (f32[64,2]{1,0:T(8,128)S(1)}, f32[64,2]{1,0:T(8,128)S(1)}, u32[]{:S(2)}, u32[]{:S(2)}) collective-permute-start(f32[64,2]{1,0:T(8,128)S(1)} %add.63), channel_id=1, source_target_pairs={{0,2},{1,3},{2,0},{3,1},{4,6},{5,7},{6,4},{7,5},{8,10},{9,11},{10,... | collective-permute-start | bytes 1544 | tf_op jit(solution)/shard_map/ppermute | solution.py:39
  64.1 19.4 %copy-start.5 = (f32[27,128]{1,0:T(8,128)S(1)}, f32[27,128]{1,0:T(8,128)}, u32[]{:S(2)}) copy-start(f32[27,128]{1,0:T(8,128)} %param.19) | copy-start | bytes 41476
  64.1 1.4 %collective-permute-start.12 = (f32[128,256]{1,0:T(8,128)S(1)}, f32[128,256]{1,0:T(8,128)S(1)}, u32[]{:S(2)}, u32[]{:S(2)}) collective-permute-start(f32[128,256]{1,0:T(8,128)S(1)} %constant_dynamic-slice_fusion), channel_id=1, source_target_pairs={{0,16},{16,0},{1,17},{17,1},{2,18},{18,2},{3,19},{19,3},{4,20},{20... | collective-permute-start | bytes 393224 | tf_op jit(solution)/shard_map/ppermute | solution.py:45
  65.6 5.6 %collective-permute-start.13 = (f32[128,256]{1,0:T(8,128)S(1)}, f32[128,256]{1,0:T(8,128)S(1)}, u32[]{:S(2)}, u32[]{:S(2)}) collective-permute-start(f32[128,256]{1,0:T(8,128)S(1)} %dynamic-slice_add_fusion), channel_id=1, source_target_pairs={{0,4},{4,0},{8,12},{12,8},{1,5},{5,1},{9,13},{13,9},{2,6},{6,2},{1... | collective-permute-start | bytes 393224 | tf_op jit(solution)/shard_map/ppermute | solution.py:39
  71.2 5.1 %collective-permute-start.14 = (f32[128,256]{1,0:T(8,128)S(1)}, f32[128,256]{1,0:T(8,128)S(1)}, u32[]{:S(2)}, u32[]{:S(2)}) collective-permute-start(f32[128,256]{1,0:T(8,128)S(1)} %add.68), channel_id=1, source_target_pairs={{0,8},{4,12},{8,0},{12,4},{1,9},{5,13},{9,1},{13,5},{2,10},{6,14},... | collective-permute-start | bytes 393224 | tf_op jit(solution)/shard_map/ppermute | solution.py:39
  76.3 5.0 %collective-permute-start.15 = (f32[128,256]{1,0:T(8,128)S(1)}, f32[128,256]{1,0:T(8,128)S(1)}, u32[]{:S(2)}, u32[]{:S(2)}) collective-permute-start(f32[128,256]{1,0:T(8,128)S(1)} %add.69), channel_id=1, source_target_pairs={{0,1},{1,0},{2,3},{3,2},{4,5},{5,4},{6,7},{7,6},{8,9},{9,8},{10,11... | collective-permute-start | bytes 393224 | tf_op jit(solution)/shard_map/ppermute | solution.py:39
  81.3 7.0 %collective-permute-start.16 = (f32[128,256]{1,0:T(8,128)S(1)}, f32[128,256]{1,0:T(8,128)S(1)}, u32[]{:S(2)}, u32[]{:S(2)}) collective-permute-start(f32[128,256]{1,0:T(8,128)S(1)} %add.70), channel_id=1, source_target_pairs={{0,2},{1,3},{2,0},{3,1},{4,6},{5,7},{6,4},{7,5},{8,10},{9,11},{10,... | collective-permute-start | bytes 393224 | tf_op jit(solution)/shard_map/ppermute | solution.py:39
  82.8 5.6 %collective-permute-start.18 = (f32[64,4]{1,0:T(8,128)S(1)}, f32[64,4]{1,0:T(8,128)S(1)}, u32[]{:S(2)}, u32[]{:S(2)}) collective-permute-start(f32[64,4]{1,0:T(8,128)S(1)} %get-tuple-element.19), channel_id=1, source_target_pairs={{0,16},{16,0},{1,17},{17,1},{2,18},{18,2},{3,19},{19,3},{4,20},{20... | collective-permute-start | bytes 3080 | tf_op jit(solution)/shard_map/ppermute | solution.py:39
  88.4 1.4 %collective-permute-start.17 = (f32[128,256]{1,0:T(8,128)S(1)}, f32[128,256]{1,0:T(8,128)S(1)}, u32[]{:S(2)}, u32[]{:S(2)}) collective-permute-start(f32[128,256]{1,0:T(8,128)S(1)} %add.71), channel_id=1, source_target_pairs={{0,16},{16,0},{1,17},{17,1},{2,18},{18,2},{3,19},{19,3},{4,20},{20... | collective-permute-start | bytes 393224 | tf_op jit(solution)/shard_map/ppermute | solution.py:45
  (5 other events, 15.3 us)
where the time goes:
time: 103 us
  waiting for transfers between devices  35 us (34%)
  starting transfers between devices  34.1 us (33%)
  local copies, waits for them, and re-layouts  11.2 us (11%)
  between operations  8.02 us (8%)
  other arithmetic  8 us (8%)
  Pallas kernels  6.19 us (6%)
    ppermute x9, waiting for transfers between devices, swapped_sum(): u = u + lax.ppermute(u, axis, [(i, i ^ step) for i in range(count)])  30.1 us
    ppermute x4, starting transfers between devices, extended(): lax.ppermute(tail, axis, [(i, (i + 1) % count) for i in range(ends)])  17.3 us
    ppermute x9, starting transfers between devices, swapped_sum(): u = u + lax.ppermute(u, axis, [(i, i ^ step) for i in range(count)])  11.5 us
    ppermute x4, starting transfers between devices, extended(): lax.ppermute(head, axis, [((i + 1) % count, i) for i in range(ends)])  5.17 us
    pallas_call x1, Pallas kernels, per_device(): vmem_call(backward, (shape((3 * C2 + 2 * C1, 8 * C1), F32), shape((C2, he...  4.21 us
    unnamed x30, local copies, waits for them, and re-layouts  2.82 us
    ppermute x4, waiting for transfers between devices, extended(): lax.ppermute(head, axis, [((i + 1) % count, i) for i in range(ends)])  2.76 us
    another operation x4, local copies, waits for them, and re-layouts, per_device(): first = jnp.stack((conv1_w, dir1.astype(BF16))).reshape(2, 9, 3, C1, C0)  2.15 us
  transfers between devices with their start and end apart: 19, of which 10 were waited for; matrix products, arithmetic and copies ran while one was open for 11% of the time, Pallas kernels for 0%

commit v1 on v0

v1 whole, which is shorter than its diff:
```python
import jax
import jax.numpy as jnp
from jax import lax
from jax.experimental import pallas as pl
from jax.experimental.pallas import tpu as pltpu
from jax.sharding import PartitionSpec as P

C0 = 4
C1 = 32
C2 = 64
ROWS = 16
REACH = 3
PIECE = 16
Q = 4
VMEM_LIMIT = 24 * 1024 * 1024
F32 = jnp.float32
BF16 = jnp.bfloat16
MESH = pl.DeviceIdType.MESH
NT = (((1,), (1,)), ((), ()))
AXES = ("dp", "gx", "gy")


def silu_parts(z):
    s = 1.0 / (1.0 + jnp.exp(-z))
    return (z * s, s * (1.0 + z * (1.0 - s)), s * (1.0 - s) * (2.0 + z * (1.0 - 2.0 * s)))


def window(ref, cells, taps=range(9)):
    columns = []
    for x, y in cells:
        columns.append(jnp.concatenate([ref[x + tap // 3, y + tap % 3] for tap in taps], axis=0))
    return jnp.concatenate(columns, axis=1)


def iota(shape, dim):
    return lax.broadcasted_iota(jnp.int32, shape, dim)


def channel_pick(rows_inside):
    inside = iota((C2, C2), 0 if rows_inside else 1)
    o = iota((C2, C2), 1 if rows_inside else 0)
    return inside == (o % Q) * (C2 // Q) + o // Q


def column_of(row, pick):
    return jnp.sum(jnp.where(pick, row, 0.0), axis=1, keepdims=True)


def row_of(column, pick):
    return jnp.sum(jnp.where(pick, column, 0.0), axis=0, keepdims=True)


def lanes_from(blocks, width):
    lane = iota(blocks[0].shape, 1)
    out = blocks[-1]
    for j in range(len(blocks) - 2, -1, -1):
        out = jnp.where(lane < (j + 1) * width, blocks[j], out)
    return out


def rolled(u, amount):
    amount %= u.shape[1]
    return pltpu.roll(u, amount, 1) if amount else u


def first_tables():
    wide = 9 * ROWS
    k = iota((32, wide), 0)
    col = iota((32, wide), 1)
    place = (col % ROWS) // C0
    c = jnp.where(place == 0, 1, jnp.where(place == 1, 0, 2))
    spread = jnp.where((place < 3) & (k == 3 * (col // ROWS) + c), 1.0, 0.0).astype(BF16)
    match = (iota((C0 * C1, wide), 0) % C0) == (iota((C0 * C1, wide), 1) % C0)
    fold = jnp.where(iota((C1, C0 * C1), 1) // C0 == iota((C1, C0 * C1), 0), 1.0, 0.0).astype(BF16)
    return spread, match, fold


def lane_of(shape):
    return lax.broadcasted_iota(jnp.int32, shape, len(shape) - 1)


def from_left(u):
    return jnp.where(lane_of(u.shape) == 0, 0.0, pltpu.roll(u, 1, 1))


def from_right(u):
    last = u.shape[1] - 1
    return jnp.where(lane_of(u.shape) == last, 0.0, pltpu.roll(u, last, 1))


def gathered(y, n):
    return from_left(y[:n]) + y[n : 2 * n] + from_right(y[2 * n : 3 * n])


def shifted(ref, cells):
    columns = []
    for x, y in cells:
        u = ref[x, y]
        columns.append(jnp.concatenate([from_right(u), u, from_left(u)], axis=0).astype(BF16))
    return jnp.concatenate(columns, axis=1)


def steps_out(size):
    found = []
    left = REACH
    while left > 0:
        found.append((len(found) + 1, min(size, left)))
        left -= size
    return found


def spans(size):
    found = [(0, 0, REACH, size)]
    for far, count in steps_out(size):
        found.append((far, size - count, REACH - (far - 1) * size - count, count))
        found.append((-far, 0, REACH + far * size, count))
    return found


def pairs_of(cells):
    return [cells[k : k + 2] for k in range(0, len(cells), 2)]


def step_kernel(
    counts, total_cells, batch, stride, per,
    v_hbm, tgt_hbm, w1_hbm, b1_hbm, w2_hbm, b2_hbm, hw_hbm, hb_hbm, k1_hbm, k2_hbm, dh_hbm,
    h_ref, hd_ref, quad_ref, field_ref,
    vin, tgt, w1, b1_in, w2, b2_in, hw_in, hb_in, k1, k2, dh_in,
    vraw, v16, a_ref, ta_ref, d_ref, p_ref, q_ref, g_ref, tg_ref, l2_ref, lb_ref, mb_ref, ms_ref, d2_ref,
    quad_src, quads, pool_src, pools, tgts, hs, rs, ag_src,
    in_sem, v_send, v_recv, pool_send, pool_recv, tgt_send, tgt_recv, rs_send, rs_recv, ag_send, ag_recv, quad_send, quad_recv,
):
    n_dp, n_x, n_y = counts
    n_all = n_dp * n_x * n_y
    _, nx, ny, lanes = vin.shape
    loads = [
        pltpu.make_async_copy(src, dst, in_sem.at[k])
        for k, (src, dst) in enumerate(
            (
                (v_hbm, vin), (w2_hbm, w2), (k2_hbm, k2), (w1_hbm, w1), (k1_hbm, k1), (tgt_hbm, tgt),
                (b1_hbm, b1_in), (b2_hbm, b2_in), (hw_hbm, hw_in), (hb_hbm, hb_in), (dh_hbm, dh_in),
            )
        )
    ]
    for load in loads:
        load.start()

    me_d, me_x, me_y = [lax.axis_index(name) for name in AXES]
    me = (me_d * n_x + me_x) * n_y + me_y

    def coords(flat):
        return (flat // (n_x * n_y), lax.rem(flat // n_y, n_x), lax.rem(flat, n_y))

    def each_other(body):
        if n_all <= 32:
            for r in range(1, n_all):
                body(lax.rem(me + r, n_all))
        else:
            lax.fori_loop(1, n_all, lambda r, c: (body(lax.rem(me + r, n_all)), c)[1], 0)

    barrier = pltpu.get_barrier_semaphore()
    each_other(lambda other: pl.semaphore_signal(barrier, inc=1, device_id=coords(other), device_id_type=MESH))

    def remote(src, dst, send, recv, where):
        return pltpu.make_async_remote_copy(
            src_ref=src, dst_ref=dst, send_sem=send, recv_sem=recv, device_id=where, device_id_type=MESH
        )

    loads[0].wait()
    for x in range(nx):
        planes = [vin[c, x].astype(F32) for c in range(C0)]
        for y in range(ny):
            vraw[REACH + x, REACH + y] = jnp.concatenate([u[y : y + 1] for u in planes], axis=0).astype(BF16)
    for load in loads[1:]:
        load.wait()

    part = C2 // Q
    for kind, ref in enumerate((w2, k2)):
        for c in range(3):
            for g in range(3):
                taps = range(4 * g, min(4 * g + 4, 9))
                rows = [ref[3 * t + c : 3 * t + c + 1, :].astype(F32).reshape(part, Q * C1) for t in taps]
                if kind:
                    for t, u in zip(taps, rows):
                        d2_ref[3 * t + c] = u
                for q in range(Q):
                    block = lanes_from([rolled(u, C1 * (j - q)) for j, u in enumerate(rows)], C1)
                    if len(rows) == 1:
                        block = block[:, :C1]
                    at = (kind * 3 + c) * C2 + q * part
                    l2_ref[at : at + part, 4 * g * C1 : 4 * g * C1 + block.shape[1]] = block.astype(BF16)

    pl.semaphore_wait(barrier, n_all - 1)

    moves = []
    for dx, sx, tx, cx in spans(nx):
        for dy, sy, ty, cy in spans(ny):
            if dx or dy:
                moves.append((dx, dy, sx, tx, cx, sy, ty, cy))

    def inside(dx, dy):
        x, y = me_x + dx, me_y + dy
        return (x >= 0) & (x < n_x) & (y >= 0) & (y < n_y)

    def halo(k):
        dx, dy, sx, tx, cx, sy, ty, cy = moves[k]
        return remote(
            vraw.at[pl.ds(REACH + sx, cx), pl.ds(REACH + sy, cy)], vraw.at[pl.ds(tx, cx), pl.ds(ty, cy)],
            v_send.at[k], v_recv.at[k], (me_d, me_x + dx, me_y + dy),
        )

    for k, (dx, dy, *_) in enumerate(moves):
        @pl.when(inside(dx, dy))
        def _():
            halo(k).start()

    def to_partner(r):
        other = lax.rem(me_d + r, n_dp)
        return remote(tgt, tgts.at[me_d], tgt_send.at[r], tgt_recv.at[r], (other, me_x, me_y))

    for r in range(1, n_dp):
        to_partner(r).start()
    tgts[me_d] = tgt[...]

    for kind in range(2):
        for c in range(3):
            rows = l2_ref[(kind * 3 + c) * C2 : (kind * 3 + c + 1) * C2, :].astype(F32)
            at = (kind * 3 + 2 - c) * C1
            both = jnp.concatenate([rows[:, :128], rows[:, 128:256]], axis=0).T
            for m in range(4):
                lb_ref[at : at + C1, 128 * m : 128 * m + 128] = both[C1 * m : C1 * m + C1].astype(BF16)
            lb_ref[at : at + C1, 512:] = rows[:, 256:].T.astype(BF16)
    back = [8 - t for t in (0, 4, 1, 5, 2, 6, 3, 7, 8)]

    spread, match, fold = first_tables()
    l1 = []
    high = k1[...].astype(BF16)
    for flat in (w1[...], high, (k1[...] - high.astype(F32)).astype(BF16)):
        flat = jnp.concatenate([flat.astype(F32), jnp.zeros((5, C0 * C1), F32)], axis=0)
        wide = jnp.dot(flat.T.astype(BF16), spread, preferred_element_type=F32)
        wide = jnp.where(match, wide, 0.0).astype(BF16)
        l1.append(jnp.dot(fold, wide, preferred_element_type=F32))
    d1 = l1[1] + l1[2]
    l1 = jnp.concatenate(l1[:2], axis=0).astype(BF16)
    b1 = column_of(b1_in[...], iota((C1, C1), 0) == iota((C1, C1), 1))
    inside_rows = channel_pick(True)
    outside_rows = channel_pick(False)
    b2 = column_of(b2_in[...], inside_rows)
    outs = hw_in.shape[0]
    square = iota((C2, C2), 0) == iota((C2, C2), 1)

    def moved_rows(whole, pick):
        return jnp.concatenate(
            [row_of(column_of(whole[m : m + 1], pick), square) for m in range(outs)], axis=0
        )

    def head_rows(ref):
        return moved_rows(ref[...], inside_rows)

    hw, dh = head_rows(hw_in), head_rows(dh_in)
    small = iota((outs, outs), 0) == iota((outs, outs), 1)
    hb = column_of(hb_in[...], small)

    def arrive(near):
        for k, (dx, dy, sx, tx, cx, sy, ty, cy) in enumerate(moves):
            if (abs(dx) <= 1 and abs(dy) <= 1) == near:
                came = inside(-dx, -dy)

                @pl.when(came)
                def _():
                    halo(k).wait_recv()

                @pl.when(jnp.logical_not(came))
                def _():
                    vraw[tx : tx + cx, ty : ty + cy] = jnp.zeros((cx, cy, C0, lanes), BF16)

    sub = iota((8, lanes), 0)

    def expand(cells):
        for x, y in cells:
            u = vraw[x, y].astype(F32)
            full = jnp.concatenate([u, u], axis=0)
            top = jnp.where(sub < C0, full, from_left(full))
            low = jnp.where(sub < C0, from_right(full), 0.0)
            v16[x, y] = jnp.concatenate([top, low], axis=0).astype(BF16)

    def valid(x, y):
        gx, gy = me_x * nx + x, me_y * ny + y
        return jnp.where((gx >= 0) & (gx < n_x * nx) & (gy >= 0) & (gy < n_y * ny), 1.0, 0.0).astype(F32)

    def first_block(cells):
        for pair in pairs_of(cells):
            res = jnp.dot(l1, window(v16, pair), preferred_element_type=F32)
            for k, (x, y) in enumerate(pair):
                part = res[:, k * lanes : (k + 1) * lanes]
                t1 = part[C1:]
                act, slope, bend = silu_parts(part[:C1] + b1)
                mine = 2 <= x < nx + 2 and 2 <= y < ny + 2
                if mine:
                    a_ref[x, y] = act.astype(BF16)
                    ta_ref[x, y] = (slope * t1).astype(BF16)
                    d_ref[0, x - 2, y - 2] = slope
                    d_ref[1, x - 2, y - 2] = bend * t1
                else:
                    mask = valid(x - 2, y - 2)
                    a_ref[x, y] = (act * mask).astype(BF16)
                    ta_ref[x, y] = (slope * t1 * mask).astype(BF16)

    n2 = 3 * C2

    def second_block(cells, sums):
        for pair in pairs_of(cells):
            res = jnp.dot(l2_ref[...], window(a_ref, pair), preferred_element_type=F32)
            tres = res[n2:] + jnp.dot(l2_ref[:n2], window(ta_ref, pair), preferred_element_type=F32)
            for k, (x, y) in enumerate(pair):
                z2 = gathered(res[:n2, k * lanes : (k + 1) * lanes], C2) + b2
                t2 = gathered(tres[:, k * lanes : (k + 1) * lanes], C2)
                act, slope, bend = silu_parts(z2)
                if sums is not None:
                    sums = (sums[0] + act, sums[1] + slope * t2)
                    p_ref[x, y] = slope
                    q_ref[x, y] = bend * t2
                else:
                    mask = valid(x - 1, y - 1)
                    p_ref[x, y] = slope * mask
                    q_ref[x, y] = bend * t2 * mask
        return sums

    def box(x0, x1, y0, y1):
        return [(x, y) for x in range(x0, x1) for y in range(y0, y1)]

    near_v = box(1, nx + 5, 1, ny + 5)
    far_v = [c for c in box(0, nx + 6, 0, ny + 6) if c not in near_v]
    near_a = box(1, nx + 3, 1, ny + 3)
    far_a = [c for c in box(0, nx + 4, 0, ny + 4) if c not in near_a]
    own_z = box(1, nx + 1, 1, ny + 1)
    far_z = [c for c in box(0, nx + 2, 0, ny + 2) if c not in own_z]

    arrive(True)
    expand(near_v)
    first_block(near_a)
    zero = jnp.zeros((C2, lanes), F32)
    sums = second_block(own_z, (zero, zero))
    row = jnp.sum(jnp.concatenate(sums, axis=0).T, axis=0, keepdims=True)
    pool_src[...] = row

    def pool_to(other):
        return remote(pool_src, pools.at[me], pool_send, pool_recv, coords(other))

    each_other(lambda other: pool_to(other).start())
    pools[me] = row

    arrive(False)
    expand(far_v)
    first_block(far_a)
    second_block(far_z, None)

    cut = 8 * C1
    m_most = jnp.zeros((2 * n2, cut), F32)
    m_rest = jnp.zeros((C1, 2 * n2), F32)
    n_most = jnp.zeros((n2, cut), F32)
    n_rest = jnp.zeros((C1, n2), F32)
    for pair in pairs_of(own_z):
        gs = shifted(p_ref, pair)
        both = jnp.concatenate([shifted(q_ref, pair), gs], axis=0)
        u = window(a_ref, pair)
        m_most = m_most + lax.dot_general(both, u[:cut], NT, preferred_element_type=F32)
        m_rest = m_rest + lax.dot_general(u[cut:], both, NT, preferred_element_type=F32)
        u = window(ta_ref, pair)
        n_most = n_most + lax.dot_general(gs, u[:cut], NT, preferred_element_type=F32)
        n_rest = n_rest + lax.dot_general(u[cut:], gs, NT, preferred_element_type=F32)
    for ref, most, rest in (
        (mb_ref, m_most[:n2] + n_most, m_rest[:, :n2] + n_rest),
        (ms_ref, m_most[n2:], m_rest[:, n2:]),
    ):
        rest = rest.T
        for c in range(3):
            rows = [most[c * C2 + q * part : c * C2 + (q + 1) * part] for q in range(Q)]
            for t in range(8):
                cols = slice(128 * (t // 4), 128 * (t // 4) + 128)
                ref[3 * t + c] = lanes_from([rolled(u[:, cols], C1 * (q - t % 4)) for q, u in enumerate(rows)], C1)
            rows = [rest[c * C2 + q * part : c * C2 + (q + 1) * part] for q in range(Q)]
            ref[24 + c] = jnp.concatenate(rows, axis=1)

    def wait_many(buf, count, sem):
        part = buf.at[pl.ds(0, count)]
        pltpu.make_async_copy(part, part, sem).wait()

    wait_many(pools, n_all - 1, pool_recv)
    for r in range(1, n_dp):
        to_partner(r).wait_recv()

    hd = jnp.zeros((outs, C2), F32)
    dpool = jnp.zeros((1, C2), F32)
    tdpool = jnp.zeros((1, C2), F32)
    group = n_x * n_y
    for d in range(n_dp):
        pair = jnp.sum(pools[d * group : (d + 1) * group], axis=0) / total_cells
        pooled, tpooled = pair[:, :C2], pair[:, C2:]
        out = jnp.sum(hw * pooled, axis=1, keepdims=True) + hb
        tout = jnp.sum(hw * tpooled + dh * pooled, axis=1, keepdims=True)
        dy = (out - column_of(tgts[d], small)) / batch
        tdy = tout / batch
        hd = hd + (tpooled * dy + pooled * tdy)
        dp = jnp.sum(dy * hw, axis=0, keepdims=True) / total_cells
        tdp = jnp.sum(tdy * hw + dy * dh, axis=0, keepdims=True) / total_cells
        dpool = jnp.where(me_d == d, dp, dpool)
        tdpool = jnp.where(me_d == d, tdp, tdpool)

    dcol, tcol = column_of(dpool, square), column_of(tdpool, square)

    def tile_of(column):
        return lanes_from(
            [jnp.broadcast_to(column[q * part : (q + 1) * part], (part, Q * C1)) for q in range(Q)], C1
        )

    dtile, ttile = tile_of(dcol), tile_of(tcol)
    owners = hs.shape[0]
    early = 27 // per

    def part_to(j):
        return remote(hs.at[j], rs.at[me], rs_send, rs_recv, coords(j * stride))

    def put(piece, block):
        at = piece % per * PIECE
        hs[piece // per, at : at + PIECE] = block.astype(BF16)

    def send_parts(first, last):
        for j in range(first, last):
            @pl.when(me != j * stride)
            def _():
                part_to(j).start()

    quad = jnp.zeros((PIECE, 128), F32)
    for k in range(27):
        term = mb_ref[k] * dtile + ms_ref[k] * ttile
        put(k, term)
        quad = quad + term * d2_ref[k]
    send_parts(0, early)

    for x, y in box(0, nx + 2, 0, ny + 2):
        slope = p_ref[x, y]
        g_ref[x, y] = (slope * dcol).astype(BF16)
        tg_ref[x, y] = (q_ref[x, y] * dcol + slope * tcol).astype(BF16)

    n1 = 3 * C1
    h1 = jnp.zeros((C1, 9 * ROWS), F32)
    for pair in pairs_of(box(0, nx, 0, ny)):
        res = jnp.dot(lb_ref[...], window(g_ref, pair, back), preferred_element_type=F32)
        tres = res[n1:] + jnp.dot(lb_ref[:n1], window(tg_ref, pair, back), preferred_element_type=F32)
        grads = []
        for k, (x, y) in enumerate(pair):
            da = gathered(res[:n1, k * lanes : (k + 1) * lanes], C1)
            tda = gathered(tres[:, k * lanes : (k + 1) * lanes], C1)
            field_ref[:, x, y, :] = tda * total_cells
            grads.append((d_ref[1, x, y] * da + d_ref[0, x, y] * tda).astype(BF16))
        around = [(x + 2, y + 2) for x, y in pair]
        h1 = h1 + lax.dot_general(
            jnp.concatenate(grads, axis=1), window(v16, around), NT, preferred_element_type=F32
        )
    own1 = jnp.sum(d1 * h1, axis=0, keepdims=True)
    tail1 = jnp.concatenate([own1[:, 128:], jnp.zeros((1, 256 - 9 * ROWS), F32)], axis=1)
    quad = jnp.sum(quad, axis=0, keepdims=True) + own1[:, :128] + tail1
    quad_src[...] = quad
    wide = lax.dot_general(fold, h1.astype(BF16), (((0,), (0,)), ((), ())), preferred_element_type=F32)
    wide = jnp.where(match, wide, 0.0).astype(BF16)
    flat = lax.dot_general(spread, wide, NT, preferred_element_type=F32)
    for k in range(27, owners * per):
        put(k, flat[(k - 27) * PIECE : (k - 26) * PIECE] if k < 29 else jnp.zeros((PIECE, 128), F32))
    send_parts(early, owners)

    def quad_to(other):
        return remote(quad_src, quads.at[me], quad_send, quad_recv, coords(other))

    each_other(lambda other: quad_to(other).start())
    quads[me] = quad

    hd_ref[...] = moved_rows(hd, outside_rows)

    def head_row(u):
        return jnp.concatenate([jnp.sum(u, axis=0, keepdims=True), jnp.zeros((1, 128 - C2), F32)], axis=1)


    slot = me // stride
    is_owner = lax.rem(me, stride) == 0
    if owners * stride != n_all:
        is_owner = is_owner & (slot < owners)

    def total_to(other):
        return remote(ag_src, h_ref.at[slot], ag_send, ag_recv, coords(other))

    def own():
        wait_many(rs, n_all - 1, rs_recv)
        rs[me] = hs[slot]
        terms = [rs[k].astype(F32) for k in range(n_all)]
        while len(terms) > 1:
            terms = [sum(terms[k : k + 2]) for k in range(0, len(terms), 2)]
        mine = terms[0].astype(BF16)
        ag_src[...] = mine
        each_other(lambda other: total_to(other).start())
        h_ref[slot] = mine
        wait_many(h_ref, owners - 1, ag_recv)
        wait_many(hs, owners - 1, rs_send)
        wait_many(rs, n_all - 1, ag_send)

    def rest_of():
        wait_many(h_ref, owners, ag_recv)
        wait_many(hs, owners, rs_send)

    if owners == n_all:
        own()
    else:
        pl.when(is_owner)(own)
        pl.when(jnp.logical_not(is_owner))(rest_of)

    for k, (dx, dy, *_) in enumerate(moves):
        @pl.when(inside(dx, dy))
        def _():
            halo(k).wait_send()

    for r in range(1, n_dp):
        to_partner(r).wait_send()
    wait_many(pools, n_all - 1, pool_send)
    wait_many(quads, n_all - 1, quad_recv)
    wait_many(quads, n_all - 1, quad_send)
    quad_ref[0:1, :] = jnp.sum(quads[...], axis=0) + head_row(dh * hd)
    quad_ref[1:2, :] = head_row(dh * dh)


def last_kernel(
    per, h_ref, hd_ref, quad_ref, field_in, dir1_ref, dir2_ref,
    next1_ref, next2_ref, head_ref, ray_ref, field_out, sem,
):
    copy = pltpu.make_async_copy(field_in, field_out, sem)
    copy.start()
    h = h_ref[...].astype(F32).reshape(-1, 128)
    h1 = h[27 * PIECE : 27 * PIECE + 27]
    hd = hd_ref[...]
    dir1 = dir1_ref[...]
    rows = [h[k * PIECE : (k + 1) * PIECE].reshape(1, PIECE * 128) for k in range(27)]
    h2 = jnp.concatenate(rows, axis=0)
    dir2 = dir2_ref[...]

    def total(u):
        u = jnp.sum(u, axis=0, keepdims=True)
        return u if u.shape[1] == 128 else sum(u[:, j : j + 128] for j in range(0, u.shape[1], 128))

    def across(u):
        return jnp.sum(u, axis=1, keepdims=True)

    quad = across(quad_ref[0:1, :])
    length = across(total(dir1 * dir1) + total(dir2 * dir2) + quad_ref[1:2, :])
    head = jnp.sum(hd * hd, axis=0, keepdims=True)
    nrm = jnp.sqrt(across(total(h1 * h1) + total(h2 * h2)) + across(head) + 1e-06)
    scale = 1.0 / nrm
    next1_ref[...] = h1 * scale
    next2_ref[...] = h2 * scale
    head_ref[...] = hd * scale
    ray_ref[...] = quad / length
    copy.wait()


def per_device(
    volume, targets, conv1_w, conv1_b, conv2_w, conv2_b, head_w, head_b, dir1, dir2, dir_head
):
    nx, ny, lanes = volume.shape[2:]
    counts = tuple(lax.axis_size(name) for name in AXES)
    n_all = counts[0] * counts[1] * counts[2]
    total_cells = nx * counts[1] * ny * counts[2] * lanes
    batch = volume.shape[0] * counts[0]
    outs = head_w.shape[1]
    per = max(1, -(-29 // n_all))
    owners = -(-29 // per)
    stride = n_all // owners
    n_moves = len(spans(nx)) * len(spans(ny)) - 1
    shape = jax.ShapeDtypeStruct
    dma = pltpu.SemaphoreType.DMA
    hbm = pl.BlockSpec(memory_space=pltpu.HBM)
    args = (
        volume[0], targets, conv1_w, conv1_b[None], conv2_w, conv2_b[None], head_w.T, head_b[None], dir1, dir2, dir_head.T
    )

    args = tuple(pltpu.with_memory_space_constraint(a, pltpu.HBM) for a in args)

    def kernel(*refs):
        step_kernel(counts, total_cells, batch, stride, per, *refs)

    h, hd, quad, field = pl.pallas_call(
        kernel,
        in_specs=[hbm] * len(args),
        out_shape=(
            shape((owners, per * PIECE, 128), BF16),
            shape((outs, C2), F32),
            shape((2, 128), F32),
            shape((C1, nx, ny, lanes), F32),
        ),
        scratch_shapes=[pltpu.VMEM(a.shape, a.dtype) for a in args]
        + [
            pltpu.VMEM((nx + 6, ny + 6, C0, lanes), BF16),
            pltpu.VMEM((nx + 6, ny + 6, ROWS, lanes), BF16),
            pltpu.VMEM((nx + 4, ny + 4, C1, lanes), BF16),
            pltpu.VMEM((nx + 4, ny + 4, C1, lanes), BF16),
            pltpu.VMEM((2, nx, ny, C1, lanes), F32),
            pltpu.VMEM((nx + 2, ny + 2, C2, lanes), F32),
            pltpu.VMEM((nx + 2, ny + 2, C2, lanes), F32),
            pltpu.VMEM((nx + 2, ny + 2, C2, lanes), BF16),
            pltpu.VMEM((nx + 2, ny + 2, C2, lanes), BF16),
            pltpu.VMEM((6 * C2, 9 * C1), BF16),
            pltpu.VMEM((6 * C1, 9 * C2), BF16),
            pltpu.VMEM((27, PIECE, 128), F32),
            pltpu.VMEM((27, PIECE, 128), F32),
            pltpu.VMEM((27, PIECE, 128), F32),
            pltpu.VMEM((1, 128), F32),
            pltpu.VMEM((n_all, 1, 128), F32),
            pltpu.VMEM((1, 2 * C2), F32),
            pltpu.VMEM((n_all, 1, 2 * C2), F32),
            pltpu.VMEM((counts[0], 1, outs), F32),
            pltpu.VMEM((owners, per * PIECE, 128), BF16),
            pltpu.VMEM((n_all, per * PIECE, 128), BF16),
            pltpu.VMEM((per * PIECE, 128), BF16),
            dma((len(args),)), dma((n_moves,)), dma((n_moves,)), dma, dma, dma((counts[0],)), dma((counts[0],)),
            dma, dma, dma, dma, dma, dma,
        ],
        compiler_params=pltpu.CompilerParams(
            collective_id=0, has_side_effects=True, vmem_limit_bytes=VMEM_LIMIT
        ),
    )(*args)

    def last(*refs):
        last_kernel(per, *refs)

    vmem = pl.BlockSpec(memory_space=pltpu.VMEM)
    next1, next2, head, ray, field = pl.pallas_call(
        last,
        in_specs=[vmem] * 6,
        out_specs=(vmem, vmem, vmem, vmem, hbm),
        out_shape=(
            shape(dir1.shape, F32), shape(dir2.shape, F32), shape((outs, C2), F32), shape((1, 1), F32),
            shape(field.shape, F32),
        ),
        scratch_shapes=[dma],
        compiler_params=pltpu.CompilerParams(vmem_limit_bytes=VMEM_LIMIT),
    )(h, hd, quad, field, dir1, dir2)
    return (next1, next2, head.T, ray[0, 0], field[None])


def solution(mesh):
    return jax.shard_map(
        per_device,
        mesh=mesh,
        in_specs=(P("dp", None, "gx", "gy", None), P("dp", None)) + (P(),) * 9,
        out_specs=(P(), P(), P(), P(), P("dp", None, "gx", "gy", None)),
        check_vma=False,
    )
```

time: 103 us -> 30.6 us (0.30)
  waiting for transfers between devices: 35 us -> 0 us
  starting transfers between devices: 34.1 us -> 0 us
  Pallas kernels: 6.19 us -> 29.8 us
  local copies, waits for them, and re-layouts: 11.2 us -> 0.01 us
  other arithmetic: 8 us -> 0 us
  between operations: 8.02 us -> 0.68 us
    ppermute x19 -> x0, waiting for transfers between devices: 35 us -> none  [the longest x9 30.1 us: swapped_sum(): u = u + lax.ppermute(u, axis, [(i, i ^ step) for i in range(count)])]
    ppermute x19 -> x0, starting transfers between devices: 34.1 us -> none  [the longest x4 17.3 us: extended(): lax.ppermute(tail, axis, [(i, (i + 1) % count) for i in range(ends)])]
    pallas_call x2, Pallas kernels: 6.19 us -> 29.8 us  [the longest x1 28.3 us: per_device(): pl.pallas_call(kernel, in_specs=[hbm] * len(args), out_shape=(shape((owne...]
    reduce_sum x6 -> x0, other arithmetic: 4.65 us -> none  [the longest x1 1.4 us: per_device(): jnp.sum(dir1 * dir1) + jnp.sum(dir2 * dir2) + jnp.sum(dir_head * dir_head)]
    another operation x7 -> x0, local copies, waits for them, and re-layouts: 2.84 us -> none  [the longest x4 2.15 us: per_device(): first = jnp.stack((conv1_w, dir1.astype(BF16))).reshape(2, 9, 3, C1, C0)]
    unnamed x30 -> x4, local copies, waits for them, and re-layouts: 2.82 us -> 0.01 us
    transpose x7 -> x0, local copies, waits for them, and re-layouts: 2.13 us -> none  [the longest x2 0.87 us: per_device(): jnp.flip(second, (1, 2)).transpose(0, 2, 4, 1, 3).reshape(6 * C1, 9 * C2)]
    reshape x10 -> x0, local copies, waits for them, and re-layouts: 2.01 us -> none  [the longest x2 0.65 us: per_device(): l2 = second.transpose(0, 2, 3, 1, 4).reshape(6 * C2, 9 * C1)]
  transfers between devices with their start and end apart: 19 -> 0, of which waited for: 10 -> 0; matrix products, arithmetic and copies ran while one was open for 11% -> 0% of each run, Pallas kernels for 0% -> 0%
where the time goes in v1:
time: 30.6 us; the launch traced here: 30.4 us
  Pallas kernels  29.8 us (97%)
  between operations  0.68 us (2%)
    pallas_call x1, Pallas kernels, per_device(): pl.pallas_call(kernel, in_specs=[hbm] * len(args), out_shape=(shape((owne...  28.3 us
    pallas_call x1, Pallas kernels, per_device(): pl.pallas_call(last, in_specs=[vmem] * 6, out_specs=(vmem, vmem, vmem, vm...  1.42 us

profile of v1, /device:TPU:0, one launch (start us, length us, event | category | flops | bytes accessed | tf_op | source)
XLA Modules:
  0.0 30.4 jit_solution(5022464839221687241)
XLA Ops:
  0.6 0.0 copy-start
  0.6 0.0 copy-start.1
  0.7 28.3 %shard_map.146 = (bf16[29,16,128]{2,1,0:T(8,128)(2,1)S(1)}, f32[4,64]{1,0:T(4,128)S(1)}, f32[2,128]{1,0:T(2,128)S(1)}, f32[32,2,8,128]{3,2,1,0:T(8,128)S(1)}) custom-call(bf16[4,2,8,128]{3,2,1,0:T(8,128)(2,1)} %bitcast.9, f32[1,4]{1,0:T(1,128)} %refs_1_.1, bf16[27,128]{1,0:T(8,128)(2,1)} %refs_2_.1, f32[1,32]{1,0:T(1,128)} %bitcast.12, ...), custom_call_target="tpu_custom_call" | custom-call | tf_op jit(solution)/shard_map/pallas_call | solution.py:588
  29.0 0.0 copy-done
  29.0 0.0 copy-done.1
  29.0 1.4 %shard_map.147 = (f32[27,128]{1,0:T(8,128)}, f32[27,2048]{1,0:T(8,128)}, f32[4,64]{1,0:T(4,128)}, f32[1,1]{1,0:T(1,128)}, f32[32,2,8,128]{3,2,1,0:T(8,128)}) custom-call(bf16[29,16,128]{2,1,0:T(8,128)(2,1)S(1)} %get-tuple-element.14.refs_0_, f32[4,64]{1,0:T(4,128)S(1)} %get-tuple-element.15.refs_1_, f32[2,128]{1,0:T(2,128)S(1)} %get-tuple-element.16.refs_2_, ...), custom_call_target="tpu_custom_call" | custom-call | tf_op jit(solution)/shard_map/pallas_call | solution.py:633
Async XLA Ops:
  0.6 28.4 %copy-start = (f32[27,2048]{1,0:T(8,128)S(1)}, f32[27,2048]{1,0:T(8,128)}, u32[]{:S(2)}) copy-start(f32[27,2048]{1,0:T(8,128)} %refs_5_.1) | copy-start | bytes 663556
  0.6 28.4 %copy-start.1 = (f32[27,128]{1,0:T(8,128)S(1)}, f32[27,128]{1,0:T(8,128)}, u32[]{:S(2)}) copy-start(f32[27,128]{1,0:T(8,128)} %refs_4_.3) | copy-start | bytes 41476

commit v2 on v1

--- a/solution.py
+++ b/solution.py
@@ -21,8 +21,10 @@
 
 
 def silu_parts(z):
-    s = 1.0 / (1.0 + jnp.exp(-z))
-    return (z * s, s * (1.0 + z * (1.0 - s)), s * (1.0 - s) * (2.0 + z * (1.0 - 2.0 * s)))
+    s = 0.5 * jnp.tanh(0.5 * z) + 0.5
+    act = z * s
+    u = 1.0 - s
+    return (act, s + act * u, s * u * ((2.0 + z) - (act + act)))
 
 
 def window(ref, cells, taps=range(9)):
@@ -126,9 +128,9 @@
     v_hbm, tgt_hbm, w1_hbm, b1_hbm, w2_hbm, b2_hbm, hw_hbm, hb_hbm, k1_hbm, k2_hbm, dh_hbm,
     h_ref, hd_ref, quad_ref, field_ref,
     vin, tgt, w1, b1_in, w2, b2_in, hw_in, hb_in, k1, k2, dh_in,
-    vraw, v16, a_ref, ta_ref, d_ref, p_ref, q_ref, g_ref, tg_ref, l2_ref, lb_ref, mb_ref, ms_ref, d2_ref,
+    vraw, v16, a_ref, ta_ref, d_ref, p_ref, q_ref, g_ref, tg_ref, l2_ref, lb_ref, l2r_ref, lbr_ref, mb_ref, ms_ref, d2_ref,
     quad_src, quads, pool_src, pools, tgts, hs, rs, ag_src,
-    in_sem, v_send, v_recv, pool_send, pool_recv, tgt_send, tgt_recv, rs_send, rs_recv, ag_send, ag_recv, quad_send, quad_recv,
+    in_sem, v_send, v_recv, pool_send, pool_recv, tgt_send, tgt_recv, rs_send, rs_recv, ag_send, ag_recv, quad_send, quad_recv, round_sem,
 ):
     n_dp, n_x, n_y = counts
     n_all = n_dp * n_x * n_y
@@ -142,30 +144,67 @@
             )
         )
     ]
-    for load in loads:
-        load.start()
-
     me_d, me_x, me_y = [lax.axis_index(name) for name in AXES]
     me = (me_d * n_x + me_x) * n_y + me_y
 
     def coords(flat):
         return (flat // (n_x * n_y), lax.rem(flat // n_y, n_x), lax.rem(flat, n_y))
 
+    def ring(at, count):
+        after = [at]
+        for k in range(1, count):
+            after.append(jnp.where(at + k >= count, at + k - count, at + k))
+        return after[1:] + after[:1]
+
+    rings = ring(me_d, n_dp), ring(me_x, n_x), ring(me_y, n_y)
+
     def each_other(body):
         if n_all <= 32:
-            for r in range(1, n_all):
-                body(lax.rem(me + r, n_all))
+            everyone = [(d, x, y) for y in rings[2] for x in rings[1] for d in rings[0]]
+            for where in everyone[:-1]:
+                body(where)
         else:
-            lax.fori_loop(1, n_all, lambda r, c: (body(lax.rem(me + r, n_all)), c)[1], 0)
+            lax.fori_loop(1, n_all, lambda r, c: (body(coords(lax.rem(me + r, n_all))), c)[1], 0)
 
     barrier = pltpu.get_barrier_semaphore()
-    each_other(lambda other: pl.semaphore_signal(barrier, inc=1, device_id=coords(other), device_id_type=MESH))
+    reach_x, reach_y = len(steps_out(nx)), len(steps_out(ny))
+    rounds = round_sem.shape[0]
+
+    def inside(dx, dy):
+        x, y = me_x + dx, me_y + dy
+        return (x >= 0) & (x < n_x) & (y >= 0) & (y < n_y)
+
+    def held(at, count, reach):
+        return jnp.minimum(at, reach) + jnp.minimum(count - 1 - at, reach) + 1
+
+    def tell(sem, far_x, far_y, cores):
+        for dx in range(-far_x, far_x + 1):
+            for dy in range(-far_y, far_y + 1):
+                if dx or dy:
+                    @pl.when(inside(dx, dy))
+                    def _():
+                        for d in cores:
+                            pl.semaphore_signal(
+                                sem, inc=1, device_id=(d, me_x + dx, me_y + dy), device_id_type=MESH
+                            )
+        for d in cores[:-1]:
+            pl.semaphore_signal(sem, inc=1, device_id=(d, me_x, me_y), device_id_type=MESH)
+
+    def tell_round(k):
+        tell(round_sem.at[k], 1, 1, [me_d])
+
+    def hear_round(k):
+        pl.semaphore_wait(round_sem.at[k], held(me_x, n_x, 1) * held(me_y, n_y, 1) - 1)
+
+    tell(barrier, reach_x, reach_y, rings[0])
 
     def remote(src, dst, send, recv, where):
         return pltpu.make_async_remote_copy(
             src_ref=src, dst_ref=dst, send_sem=send, recv_sem=recv, device_id=where, device_id_type=MESH
         )
 
+    for load in loads:
+        load.start()
     loads[0].wait()
     for x in range(nx):
         planes = [vin[c, x].astype(F32) for c in range(C0)]
@@ -175,6 +214,7 @@
         load.wait()
 
     part = C2 // Q
+    lane = iota((part, Q * C1), 1)
     for kind, ref in enumerate((w2, k2)):
         for c in range(3):
             for g in range(3):
@@ -185,22 +225,24 @@
                         d2_ref[3 * t + c] = u
                 for q in range(Q):
                     block = lanes_from([rolled(u, C1 * (j - q)) for j, u in enumerate(rows)], C1)
+                    at = (kind * 3 + c) * C2 + q * part
                     if len(rows) == 1:
+                        if kind == 0:
+                            beside = rolled(rows[0], C1 - C1 * q)
+                            l2r_ref[at : at + part] = jnp.where(lane < C1, block, 0.0)[:, : 2 * C1].astype(BF16)
+                            l2r_ref[at + 3 * C2 : at + 3 * C2 + part] = beside[:, : 2 * C1].astype(BF16)
                         block = block[:, :C1]
-                    at = (kind * 3 + c) * C2 + q * part
+                        if kind == 1:
+                            l2r_ref[at : at + part, :C1] = block.astype(BF16)
                     l2_ref[at : at + part, 4 * g * C1 : 4 * g * C1 + block.shape[1]] = block.astype(BF16)
 
-    pl.semaphore_wait(barrier, n_all - 1)
+    pl.semaphore_wait(barrier, n_dp * held(me_x, n_x, reach_x) * held(me_y, n_y, reach_y) - 1)
 
     moves = []
     for dx, sx, tx, cx in spans(nx):
         for dy, sy, ty, cy in spans(ny):
             if dx or dy:
                 moves.append((dx, dy, sx, tx, cx, sy, ty, cy))
-
-    def inside(dx, dy):
-        x, y = me_x + dx, me_y + dy
-        return (x >= 0) & (x < n_x) & (y >= 0) & (y < n_y)
 
     def halo(k):
         dx, dy, sx, tx, cx, sy, ty, cy = moves[k]
@@ -221,6 +263,7 @@
     for r in range(1, n_dp):
         to_partner(r).start()
     tgts[me_d] = tgt[...]
+    tell_round(0)
 
     for kind in range(2):
         for c in range(3):
@@ -229,7 +272,13 @@
             both = jnp.concatenate([rows[:, :128], rows[:, 128:256]], axis=0).T
             for m in range(4):
                 lb_ref[at : at + C1, 128 * m : 128 * m + 128] = both[C1 * m : C1 * m + C1].astype(BF16)
-            lb_ref[at : at + C1, 512:] = rows[:, 256:].T.astype(BF16)
+            end = rows[:, 256:].T.astype(BF16)
+            none = jnp.zeros((C1, C2), BF16)
+            if kind == 0:
+                lbr_ref[at : at + C1] = jnp.concatenate([end, none], axis=1)
+                lbr_ref[at + 3 * C1 : at + 4 * C1] = jnp.concatenate([none, end], axis=1)
+            else:
+                lbr_ref[at : at + C1, :C2] = end
     back = [8 - t for t in (0, 4, 1, 5, 2, 6, 3, 7, 8)]
 
     spread, match, fold = first_tables()
@@ -310,8 +359,11 @@
 
     def second_block(cells, sums):
         for pair in pairs_of(cells):
-            res = jnp.dot(l2_ref[...], window(a_ref, pair), preferred_element_type=F32)
-            tres = res[n2:] + jnp.dot(l2_ref[:n2], window(ta_ref, pair), preferred_element_type=F32)
+            end = jnp.concatenate([window(a_ref, pair, (8,)), window(ta_ref, pair, (8,))], axis=0)
+            res = jnp.dot(l2_ref[:, : 8 * C1], window(a_ref, pair, range(8)), preferred_element_type=F32)
+            res = res + jnp.dot(l2r_ref[...], end, preferred_element_type=F32)
+            tres = jnp.dot(l2_ref[:n2, : 8 * C1], window(ta_ref, pair, range(8)), preferred_element_type=F32)
+            tres = res[n2:] + tres
             for k, (x, y) in enumerate(pair):
                 z2 = gathered(res[:n2, k * lanes : (k + 1) * lanes], C2) + b2
                 t2 = gathered(tres[:, k * lanes : (k + 1) * lanes], C2)
@@ -336,6 +388,9 @@
     own_z = box(1, nx + 1, 1, ny + 1)
     far_z = [c for c in box(0, nx + 2, 0, ny + 2) if c not in own_z]
 
+    for k in range(rounds - 1):
+        hear_round(k)
+        tell_round(k + 1)
     arrive(True)
     expand(near_v)
     first_block(near_a)
@@ -344,10 +399,11 @@
     row = jnp.sum(jnp.concatenate(sums, axis=0).T, axis=0, keepdims=True)
     pool_src[...] = row
 
-    def pool_to(other):
-        return remote(pool_src, pools.at[me], pool_send, pool_recv, coords(other))
-
-    each_other(lambda other: pool_to(other).start())
+    def pool_to(where):
+        return remote(pool_src, pools.at[me], pool_send, pool_recv, where)
+
+    hear_round(rounds - 1)
+    each_other(lambda where: pool_to(where).start())
     pools[me] = row
 
     arrive(False)
@@ -446,8 +502,11 @@
     n1 = 3 * C1
     h1 = jnp.zeros((C1, 9 * ROWS), F32)
     for pair in pairs_of(box(0, nx, 0, ny)):
-        res = jnp.dot(lb_ref[...], window(g_ref, pair, back), preferred_element_type=F32)
-        tres = res[n1:] + jnp.dot(lb_ref[:n1], window(tg_ref, pair, back), preferred_element_type=F32)
+        end = jnp.concatenate([window(g_ref, pair, back[8:]), window(tg_ref, pair, back[8:])], axis=0)
+        res = jnp.dot(lb_ref[...], window(g_ref, pair, back[:8]), preferred_element_type=F32)
+        res = res + jnp.dot(lbr_ref[...], end, preferred_element_type=F32)
+        tres = jnp.dot(lb_ref[:n1], window(tg_ref, pair, back[:8]), preferred_element_type=F32)
+        tres = res[n1:] + tres
         grads = []
         for k, (x, y) in enumerate(pair):
             da = gathered(res[:n1, k * lanes : (k + 1) * lanes], C1)
@@ -469,10 +528,10 @@
         put(k, flat[(k - 27) * PIECE : (k - 26) * PIECE] if k < 29 else jnp.zeros((PIECE, 128), F32))
     send_parts(early, owners)
 
-    def quad_to(other):
-        return remote(quad_src, quads.at[me], quad_send, quad_recv, coords(other))
-
-    each_other(lambda other: quad_to(other).start())
+    def quad_to(where):
+        return remote(quad_src, quads.at[me], quad_send, quad_recv, where)
+
+    each_other(lambda where: quad_to(where).start())
     quads[me] = quad
 
     hd_ref[...] = moved_rows(hd, outside_rows)
@@ -486,8 +545,8 @@
     if owners * stride != n_all:
         is_owner = is_owner & (slot < owners)
 
-    def total_to(other):
-        return remote(ag_src, h_ref.at[slot], ag_send, ag_recv, coords(other))
+    def total_to(where):
+        return remote(ag_src, h_ref.at[slot], ag_send, ag_recv, where)
 
     def own():
         wait_many(rs, n_all - 1, rs_recv)
@@ -497,7 +556,7 @@
             terms = [sum(terms[k : k + 2]) for k in range(0, len(terms), 2)]
         mine = terms[0].astype(BF16)
         ag_src[...] = mine
-        each_other(lambda other: total_to(other).start())
+        each_other(lambda where: total_to(where).start())
         h_ref[slot] = mine
         wait_many(h_ref, owners - 1, ag_recv)
         wait_many(hs, owners - 1, rs_send)
@@ -572,6 +631,7 @@
     per = max(1, -(-29 // n_all))
     owners = -(-29 // per)
     stride = n_all // owners
+    rounds = max(1, counts[1] - 1 - len(steps_out(nx)), counts[2] - 1 - len(steps_out(ny)))
     n_moves = len(spans(nx)) * len(spans(ny)) - 1
     shape = jax.ShapeDtypeStruct
     dma = pltpu.SemaphoreType.DMA
@@ -606,7 +666,9 @@
             pltpu.VMEM((nx + 2, ny + 2, C2, lanes), BF16),
             pltpu.VMEM((nx + 2, ny + 2, C2, lanes), BF16),
             pltpu.VMEM((6 * C2, 9 * C1), BF16),
-            pltpu.VMEM((6 * C1, 9 * C2), BF16),
+            pltpu.VMEM((6 * C1, 8 * C2), BF16),
+            pltpu.VMEM((6 * C2, 2 * C1), BF16),
+            pltpu.VMEM((6 * C1, 2 * C2), BF16),
             pltpu.VMEM((27, PIECE, 128), F32),
             pltpu.VMEM((27, PIECE, 128), F32),
             pltpu.VMEM((27, PIECE, 128), F32),
@@ -619,7 +681,7 @@
             pltpu.VMEM((n_all, per * PIECE, 128), BF16),
             pltpu.VMEM((per * PIECE, 128), BF16),
             dma((len(args),)), dma((n_moves,)), dma((n_moves,)), dma, dma, dma((counts[0],)), dma((counts[0],)),
-            dma, dma, dma, dma, dma, dma,
+            dma, dma, dma, dma, dma, dma, pltpu.SemaphoreType.REGULAR((rounds,)),
         ],
         compiler_params=pltpu.CompilerParams(
             collective_id=0, has_side_effects=True, vmem_limit_bytes=VMEM_LIMIT

time: 30.6 us -> 28.5 us (0.931)
  Pallas kernels: 29.8 us -> 27.7 us
    pallas_call x1, Pallas kernels: 28.3 us -> 26.3 us  [per_device(): pl.pallas_call(kernel, in_specs=[hbm] * len(args), out_shape=(shape((owne...]
where the time goes in v2:
time: 28.5 us; the launch traced here: 28.4 us
  Pallas kernels  27.7 us (97%)
  between operations  0.68 us (2%)
    pallas_call x1, Pallas kernels, per_device(): pl.pallas_call(kernel, in_specs=[hbm] * len(args), out_shape=(shape((owne...  26.3 us
    pallas_call x1, Pallas kernels, per_device(): pl.pallas_call(last, in_specs=[vmem] * 6, out_specs=(vmem, vmem, vmem, vm...  1.42 us

profile of v2, /device:TPU:0, one launch (start us, length us, event | category | flops | bytes accessed | tf_op | source)
XLA Modules:
  0.0 28.4 jit_solution(5453955707937823565)
XLA Ops:
  0.6 0.0 copy-start
  0.6 0.0 copy-start.1
  0.7 26.3 %shard_map.146 = (bf16[29,16,128]{2,1,0:T(8,128)(2,1)S(1)}, f32[4,64]{1,0:T(4,128)S(1)}, f32[2,128]{1,0:T(2,128)S(1)}, f32[32,2,8,128]{3,2,1,0:T(8,128)S(1)}) custom-call(bf16[4,2,8,128]{3,2,1,0:T(8,128)(2,1)} %bitcast.9, f32[1,4]{1,0:T(1,128)} %refs_1_.1, bf16[27,128]{1,0:T(8,128)(2,1)} %refs_2_.1, f32[1,32]{1,0:T(1,128)} %bitcast.12, ...), custom_call_target="tpu_custom_call" | custom-call | tf_op jit(solution)/shard_map/pallas_call | solution.py:648
  26.9 0.0 copy-done
  27.0 0.0 copy-done.1
  27.0 1.4 %shard_map.147 = (f32[27,128]{1,0:T(8,128)}, f32[27,2048]{1,0:T(8,128)}, f32[4,64]{1,0:T(4,128)}, f32[1,1]{1,0:T(1,128)}, f32[32,2,8,128]{3,2,1,0:T(8,128)}) custom-call(bf16[29,16,128]{2,1,0:T(8,128)(2,1)S(1)} %get-tuple-element.14.refs_0_, f32[4,64]{1,0:T(4,128)S(1)} %get-tuple-element.15.refs_1_, f32[2,128]{1,0:T(2,128)S(1)} %get-tuple-element.16.refs_2_, ...), custom_call_target="tpu_custom_call" | custom-call | tf_op jit(solution)/shard_map/pallas_call | solution.py:695
Async XLA Ops:
  0.6 26.3 %copy-start = (f32[27,2048]{1,0:T(8,128)S(1)}, f32[27,2048]{1,0:T(8,128)}, u32[]{:S(2)}) copy-start(f32[27,2048]{1,0:T(8,128)} %refs_5_.1) | copy-start | bytes 663556
  0.6 26.3 %copy-start.1 = (f32[27,128]{1,0:T(8,128)S(1)}, f32[27,128]{1,0:T(8,128)}, u32[]{:S(2)}) copy-start(f32[27,128]{1,0:T(8,128)} %refs_4_.3) | copy-start | bytes 41476

commit v3 on v2

--- a/solution.py
+++ b/solution.py
@@ -124,7 +124,7 @@
 
 
 def step_kernel(
-    counts, total_cells, batch, stride, per,
+    counts, total_cells, batch, middle, per,
     v_hbm, tgt_hbm, w1_hbm, b1_hbm, w2_hbm, b2_hbm, hw_hbm, hb_hbm, k1_hbm, k2_hbm, dh_hbm,
     h_ref, hd_ref, quad_ref, field_ref,
     vin, tgt, w1, b1_in, w2, b2_in, hw_in, hb_in, k1, k2, dh_in,
@@ -474,8 +474,13 @@
     owners = hs.shape[0]
     early = 27 // per
 
+    y0, width = middle
+
+    def owner_of(j):
+        return (j // (n_x * width), j // width % n_x, y0 + j % width)
+
     def part_to(j):
-        return remote(hs.at[j], rs.at[me], rs_send, rs_recv, coords(j * stride))
+        return remote(hs.at[j], rs.at[me], rs_send, rs_recv, owner_of(j))
 
     def put(piece, block):
         at = piece % per * PIECE
@@ -483,7 +488,9 @@
 
     def send_parts(first, last):
         for j in range(first, last):
-            @pl.when(me != j * stride)
+            d, x, y = owner_of(j)
+
+            @pl.when(jnp.logical_not((me_d == d) & (me_x == x) & (me_y == y)))
             def _():
                 part_to(j).start()
 
@@ -540,10 +547,8 @@
         return jnp.concatenate([jnp.sum(u, axis=0, keepdims=True), jnp.zeros((1, 128 - C2), F32)], axis=1)
 
 
-    slot = me // stride
-    is_owner = lax.rem(me, stride) == 0
-    if owners * stride != n_all:
-        is_owner = is_owner & (slot < owners)
+    slot = (me_d * n_x + me_x) * width + me_y - y0
+    is_owner = (me_y >= y0) & (me_y < y0 + width) & (slot < owners)
 
     def total_to(where):
         return remote(ag_src, h_ref.at[slot], ag_send, ag_recv, where)
@@ -566,11 +571,8 @@
         wait_many(h_ref, owners, ag_recv)
         wait_many(hs, owners, rs_send)
 
-    if owners == n_all:
-        own()
-    else:
-        pl.when(is_owner)(own)
-        pl.when(jnp.logical_not(is_owner))(rest_of)
+    pl.when(is_owner)(own)
+    pl.when(jnp.logical_not(is_owner))(rest_of)
 
     for k, (dx, dy, *_) in enumerate(moves):
         @pl.when(inside(dx, dy))
@@ -628,9 +630,10 @@
     total_cells = nx * counts[1] * ny * counts[2] * lanes
     batch = volume.shape[0] * counts[0]
     outs = head_w.shape[1]
-    per = max(1, -(-29 // n_all))
+    width = max(1, counts[2] // 2)
+    middle = ((counts[2] - width) // 2, width)
+    per = -(-29 // (counts[0] * counts[1] * width))
     owners = -(-29 // per)
-    stride = n_all // owners
     rounds = max(1, counts[1] - 1 - len(steps_out(nx)), counts[2] - 1 - len(steps_out(ny)))
     n_moves = len(spans(nx)) * len(spans(ny)) - 1
     shape = jax.ShapeDtypeStruct
@@ -643,7 +646,7 @@
     args = tuple(pltpu.with_memory_space_constraint(a, pltpu.HBM) for a in args)
 
     def kernel(*refs):
-        step_kernel(counts, total_cells, batch, stride, per, *refs)
+        step_kernel(counts, total_cells, batch, middle, per, *refs)
 
     h, hd, quad, field = pl.pallas_call(
         kernel,

time: 28.5 us -> 28.4 us (level)
  no operation moved by 1% of the time
where the time goes in v3:
time: 28.4 us; the launch traced here: 28.2 us
  Pallas kernels  27.5 us (97%)
  between operations  0.68 us (2%)
    pallas_call x1, Pallas kernels, per_device(): pl.pallas_call(kernel, in_specs=[hbm] * len(args), out_shape=(shape((owne...  26.1 us
    pallas_call x1, Pallas kernels, per_device(): pl.pallas_call(last, in_specs=[vmem] * 6, out_specs=(vmem, vmem, vmem, vm...  1.42 us

profile of v3, /device:TPU:0, one launch (start us, length us, event | category | flops | bytes accessed | tf_op | source)
XLA Modules:
  0.0 28.2 jit_solution(10855311657224028616)
XLA Ops:
  0.6 0.0 copy-start
  0.6 0.0 copy-start.1
  0.7 26.1 %shard_map.146 = (bf16[15,32,128]{2,1,0:T(8,128)(2,1)S(1)}, f32[4,64]{1,0:T(4,128)S(1)}, f32[2,128]{1,0:T(2,128)S(1)}, f32[32,2,8,128]{3,2,1,0:T(8,128)S(1)}) custom-call(bf16[4,2,8,128]{3,2,1,0:T(8,128)(2,1)} %bitcast.9, f32[1,4]{1,0:T(1,128)} %refs_1_.1, bf16[27,128]{1,0:T(8,128)(2,1)} %refs_2_.1, f32[1,32]{1,0:T(1,128)} %bitcast.12, ...), custom_call_target="tpu_custom_call" | custom-call | tf_op jit(solution)/shard_map/pallas_call | solution.py:651
  26.8 0.0 copy-done
  26.8 0.0 copy-done.1
  26.8 1.4 %shard_map.147 = (f32[27,128]{1,0:T(8,128)}, f32[27,2048]{1,0:T(8,128)}, f32[4,64]{1,0:T(4,128)}, f32[1,1]{1,0:T(1,128)}, f32[32,2,8,128]{3,2,1,0:T(8,128)}) custom-call(bf16[15,32,128]{2,1,0:T(8,128)(2,1)S(1)} %get-tuple-element.14.refs_0_, f32[4,64]{1,0:T(4,128)S(1)} %get-tuple-element.15.refs_1_, f32[2,128]{1,0:T(2,128)S(1)} %get-tuple-element.16.refs_2_, ...), custom_call_target="tpu_custom_call" | custom-call | tf_op jit(solution)/shard_map/pallas_call | solution.py:698
Async XLA Ops:
  0.6 26.2 %copy-start = (f32[27,2048]{1,0:T(8,128)S(1)}, f32[27,2048]{1,0:T(8,128)}, u32[]{:S(2)}) copy-start(f32[27,2048]{1,0:T(8,128)} %refs_5_.1) | copy-start | bytes 663556
  0.6 26.2 %copy-start.1 = (f32[27,128]{1,0:T(8,128)S(1)}, f32[27,128]{1,0:T(8,128)}, u32[]{:S(2)}) copy-start(f32[27,128]{1,0:T(8,128)} %refs_4_.3) | copy-start | bytes 41476
